TPU v7x, 128 devices: a whole 4x4x4 slice. The times are simulated.
128 devices in a mesh: dp: 8 (over x, core), mp: 16 (over y, z).
Axes of the slice: x: 4, y: 4, z: 4, core: 2. Of those that a mesh axis runs over, the one named last changes fastest.
Arguments:
- tokens: bfloat16 [256, 8192], P('dp', 'mp'), may hold values from -6 to 6
- gate_up_weight: bfloat16 [2, 8192, 15360], P(None, 'mp', 'dp'), may hold values from -0.0625 to 0.0625
- down_weight: bfloat16 [15360, 8192], P('dp', 'mp'), may hold values from -0.046875 to 0.046875
- gate_up_input_factor: bfloat16 [2, 8192, 64], P(None, 'mp'), may hold values from -0.0625 to 0.0625
- gate_up_output_factor: bfloat16 [2, 64, 15360], P(None, None, 'dp'), may hold values from -0.046875 to 0.046875
- down_input_factor: bfloat16 [15360, 64], P('dp'), may hold values from -0.046875 to 0.046875
- down_output_factor: bfloat16 [64, 8192], P(None, 'mp'), may hold values from -0.0625 to 0.0625
- cotangent: bfloat16 [256, 8192], P('dp', 'mp'), may hold values from -6 to 6
Outputs:
- output: bfloat16 [256, 8192], P('dp', 'mp')
- input_grad: bfloat16 [256, 8192], P('dp', 'mp')
- grad_gate_up_lower: float32 [2, 8192, 64], P(None, 'mp')
- gate_up_output_factor_gradient: float32 [2, 64, 15360], P(None, None, 'dp')
- down_input_factor_gradient: float32 [15360, 64], P('dp')
- down_output_factor_gradient: float32 [64, 8192], P(None, 'mp')
All inputs are finite; a program needn't handle non-finite values.
Results may differ from a plain program's by a relative error of at most 0.0065.
Values may be sent and summed in bfloat16 or wider, within the bound.
A program may use at most 64 MiB of HBM per device.

v0:
```python
import jax
import jax.numpy as jnp
from jax import lax
from jax.sharding import Mesh
from jax.sharding import PartitionSpec as P

MP = ("mp_0", "mp_1")


adapter_scale = 2.0


def sent_to_all(array, axis):
    length = lax.axis_size(axis)
    return lax.all_to_all(
        jnp.broadcast_to(array[None], (length, *array.shape)), axis, 0, 0, tiled=True
    )


def joined_along(parts, dim):
    shape = list(parts.shape[1:])
    shape[dim] *= parts.shape[0]
    return jnp.moveaxis(parts, 0, dim).reshape(shape)


def gathered_copies(array, axis, dim):
    parts = sent_to_all(array, axis)
    return joined_along(parts, dim)


def cut_along(array, dim, length):
    shape = array.shape
    parts = array.reshape(*shape[:dim], length, shape[dim] // length, *shape[dim + 1 :])
    return jnp.moveaxis(parts, dim, 0)


def piece_ends(length, count):
    hop = length // count
    if hop >= 8:
        hop -= hop % 8
    return [hop * k for k in range(1, count)]


def sum_in_order(parts, axes, turns):
    shape = [lax.axis_size(a) for a in axes]
    parts = parts.reshape(*shape, *parts.shape[1:])
    parts = parts.transpose(*turns, *range(len(axes), parts.ndim))
    parts = parts.reshape(-1, *parts.shape[len(axes) :])
    for k in turns:
        parts = lax.psum_scatter(parts, axes[k], scatter_dimension=0, tiled=True)
    return parts[0]


def sum_at_once(array, axes, dim):
    parts = cut_along(array, dim, lax.axis_size(axes))
    widest = max(range(1, max(2, parts.ndim - 1)), key=lambda d: parts.shape[d])
    count, finished = (len(axes), [])
    for first, section in enumerate(
        jnp.split(parts, piece_ends(parts.shape[widest], count), axis=widest)
    ):
        if section.size:
            turns = [(first + k) % count for k in range(count)]
            finished.append(sum_in_order(section, axes, turns))
    return jnp.concatenate(finished, axis=widest - 1)


def sum_at_owner(array, axis, dim):
    parts = cut_along(array, dim, lax.axis_size(axis))
    arrived = lax.all_to_all(parts, axis, split_axis=0, concat_axis=0, tiled=True)
    return arrived.sum(axis=0)


def over_copies(array, axis):
    return sent_to_all(array, axis).sum(axis=0)


def in_one(arrays, axis):
    ravelled, at, finished = (jnp.concatenate([a.reshape(-1) for a in arrays]), 0, [])
    so_far = over_copies(ravelled, axis)
    for a in arrays:
        finished.append(so_far[at : at + a.size].reshape(a.shape))
        at += a.size
    return tuple(finished)


def contract_trailing(left, right, matmul_precision=None):
    return lax.dot_general(
        left,
        right,
        (((1,), (1,)), ((), ())),
        preferred_element_type=jnp.float32,
        precision=matmul_precision,
    )


def contract_leading(left, right, matmul_precision=None):
    return lax.dot_general(
        left,
        right,
        (((0,), (0,)), ((), ())),
        preferred_element_type=jnp.float32,
        precision=matmul_precision,
    )


def per_device(
    tokens,
    gate_up_weight,
    down_weight,
    gate_up_input_factor,
    gate_up_output_factor,
    down_input_factor,
    down_output_factor,
    cotangent,
):
    single_float = jnp.float32
    product_precision = lax.Precision.DEFAULT
    tok_rows = tokens.shape[0]
    input_rows_full = gathered_copies(tokens, "dp", 0)
    total = input_rows_full.shape[0]
    mp_rows = total // lax.axis_size(MP)
    scale_factor = total ** (-0.5)
    mp_start = lax.axis_index(MP) * mp_rows
    dp_start = lax.axis_index("dp") * tok_rows
    low_part = jnp.einsum(
        "td,kdr->tkr", input_rows_full, gate_up_input_factor, preferred_element_type=single_float
    )
    upper_widened = gate_up_output_factor.astype(single_float)
    term = jnp.einsum(
        "td,kdf->tkf", input_rows_full, gate_up_weight, preferred_element_type=single_float
    )
    low_slab = low_part
    term = term + adapter_scale * jnp.einsum("ubw,bwa->uba", low_slab, upper_widened)
    preactivation = sum_at_once(term, MP, 0)
    gate = preactivation[:, 0]
    upper = preactivation[:, 1]
    hidden_state = (jax.nn.silu(gate) * upper).astype(jnp.bfloat16)
    hidden_state_full = gathered_copies(hidden_state, MP, 0)
    low_down_part = jnp.dot(
        hidden_state_full, down_input_factor, preferred_element_type=single_float
    )
    down_widened_rows = down_output_factor.astype(single_float)
    term = jnp.dot(hidden_state_full, down_weight, preferred_element_type=single_float)
    low_slab = low_down_part
    term = term + adapter_scale * jnp.dot(low_slab, down_widened_rows)
    output = sum_at_owner(term, "dp", 0)
    output = output.astype(jnp.bfloat16)
    cot_all = gathered_copies(cotangent, "dp", 0)
    coeff_part = contract_leading(
        low_down_part, cot_all.astype(single_float), matmul_precision=product_precision
    )
    backward_down_rows = over_copies(contract_trailing(cot_all, down_output_factor), MP).astype(
        jnp.bfloat16
    )
    hidden_state_gradient = lax.psum_scatter(
        contract_trailing(cot_all, down_weight), MP, scatter_dimension=0, tiled=True
    )
    backward_row_block = lax.dynamic_slice_in_dim(backward_down_rows, mp_start, mp_rows, 0)
    hidden_state_gradient = hidden_state_gradient + adapter_scale * contract_trailing(
        backward_row_block, down_input_factor
    )
    down_input_factor_gradient = (
        adapter_scale * scale_factor * contract_leading(hidden_state_full, backward_down_rows)
    )
    sigma = jax.nn.sigmoid(gate)
    gate_back = hidden_state_gradient * upper * sigma * (1.0 + gate * (1.0 - sigma))
    up_back = hidden_state_gradient * gate * sigma
    pre_back = jnp.stack([gate_back, up_back], axis=1).astype(jnp.bfloat16)
    back_all = gathered_copies(pre_back, MP, 0)
    upper_partial = jnp.einsum("tkr,tkf->krf", low_part, back_all.astype(single_float))
    gate_up_output_factor_gradient = adapter_scale * scale_factor * lax.psum(upper_partial, MP)
    back_low_part = jnp.einsum(
        "tkf,krf->tkr", back_all, gate_up_output_factor, preferred_element_type=single_float
    )
    back_low_sum, down_coefficient = in_one((back_low_part, coeff_part), "dp")
    down_output_factor_gradient = adapter_scale * scale_factor * down_coefficient
    backward_lower_rows = back_low_sum.astype(jnp.bfloat16)
    grad_gate_up_lower = (
        adapter_scale
        * scale_factor
        * jnp.einsum(
            "qi,qps->pis", input_rows_full, backward_lower_rows, preferred_element_type=single_float
        )
    )
    input_total_sum = sum_at_owner(
        jnp.einsum("tkf,kdf->td", back_all, gate_up_weight, preferred_element_type=single_float),
        "dp",
        0,
    )
    low_rows_back = lax.dynamic_slice_in_dim(backward_lower_rows, dp_start, tok_rows, 0)
    input_total_sum = input_total_sum + adapter_scale * jnp.einsum(
        "tkr,kdr->td", low_rows_back, gate_up_input_factor, preferred_element_type=single_float
    )
    input_grad = input_total_sum.astype(jnp.bfloat16)
    return (
        output,
        input_grad,
        grad_gate_up_lower,
        gate_up_output_factor_gradient,
        down_input_factor_gradient,
        down_output_factor_gradient,
    )


def solution(mesh):
    torus = Mesh(mesh.devices.reshape(mesh.shape["dp"], 4, 4), ("dp", "mp_0", "mp_1"))
    in_specs = (
        P("dp", MP),
        P(None, MP, "dp"),
        P("dp", MP),
        P(None, MP, None),
        P(None, None, "dp"),
        P("dp", None),
        P(None, MP),
        P("dp", MP),
    )
    out_specs = (
        P("dp", MP),
        P("dp", MP),
        P(None, MP, None),
        P(None, None, "dp"),
        P("dp", None),
        P(None, MP),
    )
    return jax.shard_map(
        per_device, mesh=torus, in_specs=in_specs, out_specs=out_specs, check_vma=False
    )
```

profile of v0, /device:TPU:1, one launch (start us, length us, event | category | flops | bytes accessed | tf_op | source)
XLA Modules:
  0.0 344.0 jit_solution(7605972328173418897)
XLA Ops:
  8.1 0.9 broadcast_in_dim.12
  9.0 12.1 %all_to_all.41 = bf16[8,32,512]{2,1,0:T(8,128)(2,1)S(1)} all-to-all(bf16[8,32,512]{2,1,0:T(8,128)(2,1)S(1)} %broadcast_in_dim.12), channel_id=1, replica_groups=mesh['dp'=8,'mp_0'=4,'mp_1'=4] {'dp'}, dimensions={0} | all-to-all | bytes 524288 | tf_op jit(solution)/shard_map/all_to_all | solution.py:15
  21.0 3.4 fusion.22
  24.7 0.7 bitcast_add_fusion
  25.4 1.6 fusion.19
  26.9 1.4 copy.44
  28.4 3.0 copy.52
  31.5 0.7 copy-done.12
  32.2 9.9 %all_to_all.42 = bf16[8,32,512]{2,1,0:T(8,128)(2,1)S(1)} all-to-all(bf16[8,32,512]{2,1,0:T(8,128)(2,1)S(1)} %broadcast_in_dim.14), channel_id=1, replica_groups=mesh['dp'=8,'mp_0'=4,'mp_1'=4] {'dp'}, dimensions={0} | all-to-all | bytes 524288 | tf_op jit(solution)/shard_map/all_to_all | solution.py:15
  42.1 2.0 fusion.25
  44.2 14.0 %reduce-scatter.9.cloned.1.call-done = f32[4,8,2,1920]{3,1,2,0:T(8,128)} async-done(((f32[16,8,2,1920]{3,1,2,0:T(8,128)}), f32[4,8,2,1920]{3,1,2,0:T(8,128)}) %reduce-scatter.9.cloned.1.call-update) | async-done | bytes 491536 | tf_op jit(solution)/shard_map/reduce_scatter | solution.py:50
  58.5 1.1 broadcast_in_dim.15
  59.6 5.2 %all-to-all-start.4 = ((f32[16,256,64]{1,2,0:T(8,128)}), f32[16,256,64]{1,2,0:T(8,128)}, u32[]{:S(2)}, u32[]{:S(2)}) async-start(f32[16,256,64]{1,2,0:T(8,128)} %broadcast_in_dim.15), calls=%async_computation.8 | async-start | bytes 2097152 | tf_op jit(solution)/shard_map/all_to_all | solution.py:15
  64.8 33.5 %reduce-scatter.5.cloned.1.call-done = f32[4,8,2,1920]{3,1,2,0:T(8,128)} async-done(((f32[16,8,2,1920]{3,1,2,0:T(8,128)}), f32[4,8,2,1920]{3,1,2,0:T(8,128)}) %reduce-scatter.5.cloned.1.call-update) | async-done | bytes 491536 | tf_op jit(solution)/shard_map/reduce_scatter | solution.py:50
  99.6 1.3 reduce_sum.37
  100.9 45.5 %all-reduce.6.cloned.1.call-done = f32[256,1920]{1,0:T(8,128)} async-done(((f32[256,1920]{1,0:T(8,128)}), f32[256,1920]{1,0:T(8,128)}) %all-reduce.6.cloned.1.call-update) | async-done | bytes 1966096
  146.4 2.1 fusion.15
  148.5 1.0 broadcast_in_dim.13
  149.5 4.9 %all-to-all-start.1 = ((bf16[16,16,1920]{2,1,0:T(8,128)(2,1)}), bf16[16,16,1920]{2,1,0:T(8,128)(2,1)S(1)}, u32[]{:S(2)}, u32[]{:S(2)}) async-start(bf16[16,16,1920]{2,1,0:T(8,128)(2,1)} %broadcast_in_dim.13), calls=%async_computation.5 | async-start | bytes 1966080 | tf_op jit(solution)/shard_map/all_to_all | solution.py:15
  154.5 1.5 pad_maximum_fusion.2
  156.0 13.2 %all-to-all-done.1 = bf16[16,16,1920]{2,1,0:T(8,128)(2,1)S(1)} async-done(((bf16[16,16,1920]{2,1,0:T(8,128)(2,1)}), bf16[16,16,1920]{2,1,0:T(8,128)(2,1)S(1)}, u32[]{:S(2)}, u32[]{:S(2)}) %all-to-all-start.1) | async-done | bytes 983072 | tf_op jit(solution)/shard_map/all_to_all | solution.py:15
  169.2 2.3 broadcast_in_dim.16
  171.5 4.4 %all-to-all-start.5 = ((bf16[16,16,2,1920]{3,1,2,0:T(8,128)(2,1)}), bf16[16,16,2,1920]{3,1,2,0:T(8,128)(2,1)}, u32[]{:S(2)}, u32[]{:S(2)}) async-start(bf16[16,16,2,1920]{3,1,2,0:T(8,128)(2,1)} %broadcast_in_dim.16), calls=%async_computation.9 | async-start | bytes 3932160 | tf_op jit(solution)/shard_map/all_to_all | solution.py:15
  176.0 1.4 fusion.24
  177.5 0.7 copy.54
  178.4 1.5 convolution_add_fusion
  179.9 20.3 %all-to-all-done.5 = bf16[16,16,2,1920]{3,1,2,0:T(8,128)(2,1)} async-done(((bf16[16,16,2,1920]{3,1,2,0:T(8,128)(2,1)}), bf16[16,16,2,1920]{3,1,2,0:T(8,128)(2,1)}, u32[]{:S(2)}, u32[]{:S(2)}) %all-to-all-start.5) | async-done | bytes 1966112 | tf_op jit(solution)/shard_map/all_to_all | solution.py:15
  200.2 9.4 %all-to-all-start.2 = ((f32[8,32,512]{2,1,0:T(8,128)}), f32[8,32,512]{2,1,0:T(8,128)}, u32[]{:S(2)}, u32[]{:S(2)}) async-start(f32[8,32,512]{2,1,0:T(8,128)} %bitcast.110), calls=%async_computation.6 | async-start | bytes 1048576 | tf_op jit(solution)/shard_map/all_to_all | solution.py:69
  209.6 1.7 copy.45
  211.4 1.3 copy-done.1
  212.7 1.4 convolution_bitcast_fusion
  214.0 1.0 copy.46
  215.1 0.8 reshape.119
  215.9 4.7 %fusion.3 = f32[8,32,512]{2,1,0:T(8,128)} fusion(bf16[8,32,1920,2]{2,1,0,3:T(8,128)(2,1)} %bitcast.96, bf16[2,512,1920]{2,1,0:T(8,128)(2,1)} %param.9), kind=kOutput, calls=%fused_computation.6 | convolution fusion | flops 1006632960 | bytes 6422528 | tf_op jit(solution)/shard_map/tkf,kdf->td/dot_general | solution.py:186
  220.6 4.8 %all-to-all-start.6 = ((f32[8,32,512]{2,1,0:T(8,128)}), f32[8,32,512]{2,1,0:T(8,128)}, u32[]{:S(2)}, u32[]{:S(2)}) async-start(f32[8,32,512]{2,1,0:T(8,128)} %fusion.3), calls=%async_computation.10 | async-start | bytes 1048576 | tf_op jit(solution)/shard_map/all_to_all | solution.py:69
  225.4 1.0 pad_maximum_fusion
  226.4 8.5 %all-to-all-done.6 = f32[8,32,512]{2,1,0:T(8,128)} async-done(((f32[8,32,512]{2,1,0:T(8,128)}), f32[8,32,512]{2,1,0:T(8,128)}, u32[]{:S(2)}, u32[]{:S(2)}) %all-to-all-start.6) | async-done | bytes 524320 | tf_op jit(solution)/shard_map/all_to_all | solution.py:69
  234.9 2.4 broadcast_in_dim.17
  237.3 5.3 %all-to-all-start.7 = ((f32[8,1,65536]{2,1,0:T(1,128)}), f32[8,1,65536]{2,1,0:T(1,128)}, u32[]{:S(2)}, u32[]{:S(2)}) async-start(f32[8,1,65536]{2,1,0:T(1,128)} %broadcast_in_dim.17), calls=%async_computation.11 | async-start | bytes 4194304 | tf_op jit(solution)/shard_map/all_to_all | solution.py:15
  242.6 2.9 fusion.27
  245.6 1.1 convolution_multiply_fusion
  246.7 1.7 reduce_sum.36
  248.4 1.1 reduce_sum.38
  249.5 79.5 %all-reduce.4.cloned.1.call-done = f32[2,64,1920]{2,1,0:T(8,128)} async-done(((f32[2,64,1920]{2,1,0:T(8,128)}), f32[2,64,1920]{2,1,0:T(8,128)}) %all-reduce.4.cloned.1.call-update) | async-done | bytes 983056 | tf_op jit(solution)/shard_map/psum | solution.py:171
  328.9 2.2 broadcast_multiply_fusion
  331.1 3.2 reduce_sum.39
  334.4 0.9 fusion.6
  336.0 0.8 fusion.9
  (54 shorter events, 2.6 us)
Async XLA Ops:
  8.0 34.1 %copy-start = (bf16[1920,512]{1,0:T(8,128)(2,1)S(1)}, bf16[1920,512]{1,0:T(8,128)(2,1)}, u32[]{:S(2)}) copy-start(bf16[1920,512]{1,0:T(8,128)(2,1)} %param.10) | copy-start | bytes 5898244
  8.0 50.2 %reduce-scatter.9.cloned.1.call-start = ((), (), s32[]{:S(2)}) async-start(), calls=%async_computation.14 | async-start | bytes 2457600 | tf_op jit(solution)/shard_map/reduce_scatter | solution.py:50
  21.0 3.4 copy-start.6
  21.0 3.6 %copy-start.2 = (bf16[2,64,1920]{2,1,0:T(8,128)(2,1)S(1)}, bf16[2,64,1920]{2,1,0:T(8,128)(2,1)}, u32[]{:S(2)}) copy-start(bf16[2,64,1920]{2,1,0:T(8,128)(2,1)} %param.12) | copy-start | bytes 1474564
  24.6 0.7 copy-start.4
  28.4 69.9 %reduce-scatter.5.cloned.1.call-start = ((), (), s32[]{:S(2)}) async-start(), calls=%async_computation.12 | async-start | bytes 2457600 | tf_op jit(solution)/shard_map/reduce_scatter | solution.py:50
  31.4 0.8 copy-start.12
  31.4 115.0 %all-reduce.6.cloned.1.call-start = ((), (), s32[]{:S(2)}) async-start(), calls=%async_computation.17 | async-start | bytes 3932160
  44.1 14.1 %copy-start.8 = (bf16[64,512]{1,0:T(8,128)(2,1)S(1)}, bf16[64,512]{1,0:T(8,128)(2,1)}, u32[]{:S(2)}) copy-start(bf16[64,512]{1,0:T(8,128)(2,1)} %param.14) | copy-start | bytes 196612
  44.1 102.3 %reduce-scatter.11.cloned.1.call-start = ((), (), s32[]{:S(2)}) async-start(), calls=%async_computation.15 | async-start | bytes 614400 | tf_op jit(solution)/shard_map/reduce_scatter | solution.py:50
  58.5 39.9 %copy-start.13 = (u32[128]{0:T(128)S(1)}, u32[128]{0:T(128)}, u32[]{:S(2)}) copy-start(u32[128]{0:T(128)} %constant.41) | copy-start | bytes 1540
  59.6 86.9 %copy-start.9 = (bf16[1920,64]{0,1:T(8,128)(2,1)S(1)}, bf16[1920,64]{0,1:T(8,128)(2,1)}, u32[]{:S(2)}) copy-start(bf16[1920,64]{0,1:T(8,128)(2,1)} %param.13) | copy-start | bytes 737284
  59.6 40.0 %all-to-all-start.4 = ((f32[16,256,64]{1,2,0:T(8,128)}), f32[16,256,64]{1,2,0:T(8,128)}, u32[]{:S(2)}, u32[]{:S(2)}) async-start(f32[16,256,64]{1,2,0:T(8,128)} %broadcast_in_dim.15), calls=%async_computation.8 | async-start | bytes 2097152 | tf_op jit(solution)/shard_map/all_to_all | solution.py:15
  64.8 81.7 %reduce-scatter.7.cloned.1.call-start = ((), (), s32[]{:S(2)}) async-start(), calls=%async_computation.13 | async-start | bytes 614400 | tf_op jit(solution)/shard_map/reduce_scatter | solution.py:50
  100.9 48.6 %copy-start.10 = (bf16[256,64]{0,1:T(8,128)(2,1)}, bf16[256,64]{0,1:T(8,128)(2,1)S(1)}, u32[]{:S(2)}) copy-start(bf16[256,64]{0,1:T(8,128)(2,1)S(1)} %reduce_sum.37) | copy-start | bytes 98308
  149.5 19.7 %all-to-all-start.1 = ((bf16[16,16,1920]{2,1,0:T(8,128)(2,1)}), bf16[16,16,1920]{2,1,0:T(8,128)(2,1)S(1)}, u32[]{:S(2)}, u32[]{:S(2)}) async-start(bf16[16,16,1920]{2,1,0:T(8,128)(2,1)} %broadcast_in_dim.13), calls=%async_computation.5 | async-start | bytes 1966080 | tf_op jit(solution)/shard_map/all_to_all | solution.py:15
  171.5 28.7 %all-to-all-start.5 = ((bf16[16,16,2,1920]{3,1,2,0:T(8,128)(2,1)}), bf16[16,16,2,1920]{3,1,2,0:T(8,128)(2,1)}, u32[]{:S(2)}, u32[]{:S(2)}) async-start(bf16[16,16,2,1920]{3,1,2,0:T(8,128)(2,1)} %broadcast_in_dim.16), calls=%async_computation.9 | async-start | bytes 3932160 | tf_op jit(solution)/shard_map/all_to_all | solution.py:15
  200.2 20.4 %all-to-all-start.2 = ((f32[8,32,512]{2,1,0:T(8,128)}), f32[8,32,512]{2,1,0:T(8,128)}, u32[]{:S(2)}, u32[]{:S(2)}) async-start(f32[8,32,512]{2,1,0:T(8,128)} %bitcast.110), calls=%async_computation.6 | async-start | bytes 1048576 | tf_op jit(solution)/shard_map/all_to_all | solution.py:69
  209.6 3.0 copy-start.3
  211.4 1.3 copy-start.1
  220.6 14.3 %all-to-all-start.6 = ((f32[8,32,512]{2,1,0:T(8,128)}), f32[8,32,512]{2,1,0:T(8,128)}, u32[]{:S(2)}, u32[]{:S(2)}) async-start(f32[8,32,512]{2,1,0:T(8,128)} %fusion.3), calls=%async_computation.10 | async-start | bytes 1048576 | tf_op jit(solution)/shard_map/all_to_all | solution.py:69
  237.3 5.3 %copy-start.5 = (f32[256,128]{0,1:S(1)}, f32[256,128]{0,1}, u32[]{:S(2)}) copy-start(f32[256,128]{0,1} %copy-done.4) | copy-start | bytes 393220
  237.3 93.8 %all-to-all-start.7 = ((f32[8,1,65536]{2,1,0:T(1,128)}), f32[8,1,65536]{2,1,0:T(1,128)}, u32[]{:S(2)}, u32[]{:S(2)}) async-start(f32[8,1,65536]{2,1,0:T(1,128)} %broadcast_in_dim.17), calls=%async_computation.11 | async-start | bytes 4194304 | tf_op jit(solution)/shard_map/all_to_all | solution.py:15
  242.6 3.0 copy-start.11
  242.6 86.3 %all-reduce.4.cloned.1.call-start = ((), (), s32[]{:S(2)}) async-start(), calls=%async_computation.16 | async-start | bytes 1966080 | tf_op jit(solution)/shard_map/psum | solution.py:171
  331.1 4.9 %copy-start.7 = (bf16[2,512,64]{1,2,0:T(8,128)(2,1)S(1)}, bf16[2,512,64]{1,2,0:T(8,128)(2,1)}, u32[]{:S(2)}) copy-start(bf16[2,512,64]{1,2,0:T(8,128)(2,1)} %param.11) | copy-start | bytes 393220
Sparse Core Ops, SparseCore 0:
  28.5 29.6 reduce-scatter.8
  60.7 37.6 reduce-scatter.4
  100.7 19.1 reduce-scatter.10
  122.2 23.7 reduce-scatter.6
Sparse Core Ops, SparseCore 1:
  44.2 102.2 all-reduce.5
  247.0 81.9 all-reduce.3
where the time goes:
time: 347 us; the launch traced here: 344 us
  waiting for transfers between devices  215 us (62%)
  starting transfers between devices  34.3 us (10%)
  matrix products  23.7 us (7%)
  blocking collectives  22 us (6%)
  local copies, waits for them, and re-layouts  21.4 us (6%)
  between operations  16.1 us (5%)
  other arithmetic  12 us (3%)
    psum x1, waiting for transfers between devices, per_device(): lax.psum(upper_partial, MP)  79.5 us
    reduce_scatter x4, waiting for transfers between devices, sum_in_order(): parts = lax.psum_scatter(parts, axes[k], scatter_dimension=0, tiled=True)  47.6 us
    unnamed x7, waiting for transfers between devices  45.6 us
    all_to_all x4, waiting for transfers between devices, sent_to_all(): lax.all_to_all(jnp.broadcast_to(array[None], (length, *array.shape)), axi...  33.5 us
    all_to_all x2, blocking collectives, sent_to_all(): lax.all_to_all(jnp.broadcast_to(array[None], (length, *array.shape)), axi...  22 us
    all_to_all x4, starting transfers between devices, sent_to_all(): lax.all_to_all(jnp.broadcast_to(array[None], (length, *array.shape)), axi...  19.9 us
    all_to_all x2, starting transfers between devices, sum_at_owner(): lax.all_to_all(parts, axis, split_axis=0, concat_axis=0, tiled=True)  14.2 us
    all_to_all x2, waiting for transfers between devices, sum_at_owner(): lax.all_to_all(parts, axis, split_axis=0, concat_axis=0, tiled=True)  8.47 us
  transfers between devices with their start and end apart: 12, of which 7 were waited for; matrix products, arithmetic and copies ran while one was open for 10% of the time, Pallas kernels for 0%

commit v1 on v0

v1 whole, which is shorter than its diff:
```python
import jax
import jax.numpy as jnp
from jax import lax
from jax.experimental import pallas as pl
from jax.experimental.pallas import tpu as pltpu
from jax.sharding import Mesh
from jax.sharding import PartitionSpec as P

MESH = pl.DeviceIdType.MESH
F32 = jnp.float32
BF16 = jnp.bfloat16

X, C, Y, Z = 4, 2, 4, 4
T = 256
DS = 512
FS = 1920
R = 64
EXT = 256
SCALE = 2.0 * T ** -0.5

SUBS = (
    ("y", 0, 512, False),
    ("z", 1024, 384, True),
    ("y", 512, 512, False),
    ("z", 1408, 512, False),
)
WIDTHS = tuple(3 * hw + (EXT if ext else 0) for _, _, hw, ext in SUBS)
NS = len(SUBS)
N_SEM = 48 + 24 * NS


def nn(a, b):
    return jnp.dot(a, b, preferred_element_type=F32)


def nt(a, b):
    return lax.dot_general(a, b, (((1,), (1,)), ((), ())), preferred_element_type=F32)


def body(tok, w_hbm, wd_hbm, at_hbm, b_hbm, dint_hbm, dout_hbm, cot,
         o_out, o_in, o_gl, o_gf, o_di, o_do,
         xc, w, wd, at, bf, dint, dout, acc_o, acc_i, acc_e, qt, rt, uq, rx, eg, *rest):
    per = len(rest) - 3
    each = per // NS
    bufs = [rest[s * each:(s + 1) * each] for s in range(NS)]
    local_sem, send_sem, recv_sem = rest[per:]
    me = {a: lax.axis_index(a) for a in ("x", "c", "y", "z")}

    def at_off(axis, off):
        return lax.rem(me[axis] + off, 4)

    count = [0]
    started = []

    def put(src, dst, device):
        n = count[0]
        count[0] += 1
        c = pltpu.make_async_remote_copy(
            src_ref=src, dst_ref=dst, send_sem=send_sem.at[n], recv_sem=recv_sem.at[n],
            device_id=device, device_id_type=MESH)
        c.start()
        started.append(c)
        return c

    other = 1 - me["c"]
    barrier = pltpu.get_barrier_semaphore()
    partners = [{"c": other}]
    for off in (1, 2, 3):
        partners += [{"x": at_off("x", off)}, {"x": at_off("x", off), "c": other},
                     {"y": at_off("y", off)}, {"z": at_off("z", off)}]
    for p in partners:
        pl.semaphore_signal(barrier, inc=1, device_id=p, device_id_type=MESH)

    my_dp = me["x"] * 2 + me["c"]
    loads = []
    for n, (src, dst) in enumerate((
        (tok, xc.at[0, my_dp]), (cot, xc.at[1, my_dp]), (at_hbm, at), (dout_hbm, dout),
        (b_hbm, bf), (dint_hbm, dint), (w_hbm, w), (wd_hbm, wd),
    )):
        c = pltpu.make_async_copy(src, dst, local_sem.at[n])
        c.start()
        loads.append(c)
    loads[0].wait()
    loads[1].wait()
    pl.semaphore_wait(barrier, len(partners))

    def block(off):
        return at_off("x", off) * 2 + me["c"]

    def whole(off):
        return xc.at[:, block(off)]

    g_right = put(whole(0), whole(0), {"x": at_off("x", 1)})
    g_left = put(whole(0), whole(0), {"x": at_off("x", 3)})
    g_pair = [put(whole(0), whole(0), {"c": other})]
    g_right.wait_recv()
    f_right = put(xc.at[0, block(3)], xc.at[0, block(3)], {"x": at_off("x", 1)})
    g_left.wait_recv()
    f_left = put(xc.at[1, block(1)], xc.at[1, block(1)], {"x": at_off("x", 3)})
    g_pair.append(put(whole(3), whole(3), {"c": other}))
    g_pair.append(put(whole(1), whole(1), {"c": other}))
    for c in loads[2:]:
        c.wait()
    f_right.wait_recv()
    f_left.wait_recv()
    g_pair.append(put(whole(2), whole(2), {"c": other}))
    for c in g_pair:
        c.wait_recv()

    xs = xc[0].reshape(T, DS)
    cs = xc[1].reshape(T, DS)
    low = [nt(xs, at[k]) for k in range(2)]
    bd = nt(cs, dout[...])
    low2 = [(2.0 * v).astype(BF16) for v in low]
    bd2 = (2.0 * bd).astype(BF16)

    def seg(n, hw):
        return slice(n * hw, (n + 1) * hw)

    def compute(s):
        _, f0, hw, ext = SUBS[s]
        p, q = bufs[s][0], bufs[s][1]
        cols = slice(f0, f0 + hw)
        for n in range(3):
            if n < 2:
                v = nn(xs, w[n, :, cols]) + nn(low2[n], bf[n, :, cols])
            else:
                v = nt(cs, wd[cols, :]) + nn(bd2, dint[:, cols])
            v = v.reshape(Y, Z, 16, hw)
            p[:, :, :, seg(n, hw)] = v
            q[:, :, :, seg(n, hw)] = v.astype(BF16)
        if ext:
            v = jnp.concatenate([low[0], low[1], bd, jnp.zeros_like(bd)], axis=1)
            v = v.reshape(Y, Z, 16, EXT)
            p[:, :, :, 3 * hw:] = v
            q[:, :, :, 3 * hw:] = v.astype(BF16)

    other_axis = {"y": "z", "z": "y"}

    def part(ref, s, a1, lo, hi):
        if SUBS[s][0] == "y":
            return ref.at[a1, lo:hi]
        return ref.at[lo:hi, a1]

    def value(ref, s, a1, a2):
        if SUBS[s][0] == "y":
            return ref[a1, a2]
        return ref[a2, a1]

    st = [dict() for _ in range(NS)]

    def rs1_send(s):
        a = SUBS[s][0]
        q, tr, tl, fr, fl = bufs[s][1], bufs[s][2], bufs[s][3], bufs[s][6], bufs[s][7]
        left, right = {a: at_off(a, 3)}, {a: at_off(a, 1)}
        st[s]["t"] = [
            put(part(q, s, at_off(a, 2), 0, 2), tr, left),
            put(part(q, s, at_off(a, 2), 2, 4), tl, right),
        ]
        st[s]["f"] = [
            put(part(q, s, at_off(a, 3), 2, 4), fr.at[2:4], left),
            put(part(q, s, at_off(a, 1), 0, 2), fl.at[0:2], right),
        ]

    def rs1_agg(s):
        a = SUBS[s][0]
        p, tr, tl, gr, gl, fr, fl = (bufs[s][k] for k in (0, 2, 3, 4, 5, 6, 7))
        left, right = {a: at_off(a, 3)}, {a: at_off(a, 1)}
        st[s]["t"][0].wait_recv()
        for j in range(2):
            gr[j] = (value(p, s, at_off(a, 3), j) + tr[j].astype(F32)).astype(BF16)
        st[s]["f"].append(put(gr, fr.at[0:2], left))
        st[s]["t"][1].wait_recv()
        for j in range(2):
            gl[j] = (value(p, s, at_off(a, 1), 2 + j) + tl[j].astype(F32)).astype(BF16)
        st[s]["f"].append(put(gl, fl.at[2:4], right))

    def rs1_fin(s):
        a = SUBS[s][0]
        b = other_axis[a]
        p, fr, fl, sm, q2, r2 = (bufs[s][k] for k in (0, 6, 7, 8, 9, 10))
        for c in st[s]["f"]:
            c.wait_recv()
        for j in range(4):
            v = value(p, s, me[a], j) + fr[j].astype(F32) + fl[j].astype(F32)
            sm[j] = v
            q2[j] = v.astype(BF16)
        st[s]["r"] = [
            put(q2.at[at_off(b, off)], r2.at[off - 1], {b: at_off(b, off)})
            for off in (2, 1, 3)
        ]

    def middle(s):
        a, f0, hw, ext = SUBS[s]
        b = other_axis[a]
        sm, r2, act = (bufs[s][k] for k in (8, 10, 11))
        for c in st[s]["r"]:
            c.wait_recv()

        def total(cols):
            v = sm[me[b], :, cols]
            for n in range(3):
                v = v + r2[n, :, cols].astype(F32)
            return v

        gate, up, hb = (total(seg(n, hw)) for n in range(3))
        sg = 1.0 / (1.0 + jnp.exp(-gate))
        my = (me["y"], me["z"])
        gs = gate * sg
        act[my[0], my[1], :, seg(0, hw)] = (gs * up).astype(BF16)
        act[my[0], my[1], :, seg(1, hw)] = (hb * up * sg * (1.0 + gate * (1.0 - sg))).astype(BF16)
        act[my[0], my[1], :, seg(2, hw)] = (hb * gs).astype(BF16)
        if ext:
            act[my[0], my[1], :, 3 * hw:] = total(slice(3 * hw, 3 * hw + EXT)).astype(BF16)
        mine = act.at[my[0], my[1]]
        st[s]["a1"] = [put(mine, mine, {b: at_off(b, off)}) for off in (2, 1, 3)]

    def ag2_send(s):
        a = SUBS[s][0]
        act = bufs[s][11]
        left, right = {a: at_off(a, 3)}, {a: at_off(a, 1)}
        for c in st[s]["a1"]:
            c.wait_recv()
        lo, hi = part(act, s, me[a], 0, 2), part(act, s, me[a], 2, 4)
        st[s]["fromright"] = [put(lo, lo, left)]
        st[s]["fromleft"] = [put(hi, hi, right)]
        st[s]["fromright"].append(put(hi, hi, left))
        st[s]["fromleft"].append(put(lo, lo, right))

    def ag2_fwd(s):
        a = SUBS[s][0]
        act = bufs[s][11]
        left, right = {a: at_off(a, 3)}, {a: at_off(a, 1)}
        st[s]["fromright"][0].wait_recv()
        src = part(act, s, at_off(a, 1), 0, 2)
        st[s]["fromright"].append(put(src, src, left))
        st[s]["fromleft"][0].wait_recv()
        src = part(act, s, at_off(a, 3), 2, 4)
        st[s]["fromleft"].append(put(src, src, right))

    def ag2_fin(s):
        for c in st[s]["fromright"][1:] + st[s]["fromleft"][1:]:
            c.wait_recv()

    def act_of(s, cols):
        n = cols.stop - cols.start
        return bufs[s][11][:, :, :, cols].reshape(T, n)

    first = [True]

    def post(s):
        _, f0, hw, ext = SUBS[s]
        cols = slice(f0, f0 + hw)
        hid, gb, ub = (act_of(s, seg(n, hw)) for n in range(3))
        o = nn(hid, wd[cols, :])
        i = nt(gb, w[0, :, cols]) + nt(ub, w[1, :, cols])
        e = [nt(gb, bf[0, :, cols]), nt(ub, bf[1, :, cols]), nt(hid, dint[:, cols])]
        if first[0]:
            acc_o[...] = o
            acc_i[...] = i
            for n in range(3):
                acc_e[n] = e[n]
            first[0] = False
        else:
            acc_o[...] += o
            acc_i[...] += i
            for n in range(3):
                acc_e[n] += e[n]

    def grads():
        s = [n for n in range(NS) if SUBS[n][3]][0]
        hw = SUBS[s][2]
        ext = act_of(s, slice(3 * hw, 3 * hw + EXT)).astype(F32)
        ext_t = jnp.transpose(ext).astype(BF16)
        for s in range(NS):
            _, f0, hw, _ = SUBS[s]
            cols = slice(f0, f0 + hw)
            for k in range(2):
                o_gf[k, :, cols] = SCALE * nn(ext_t[64 * k:64 * k + 64], act_of(s, seg(1 + k, hw)))
            o_di[:, cols] = SCALE * nn(ext_t[128:192], act_of(s, seg(0, hw)))

    order = range(NS)
    compute(0)
    rs1_send(0)
    compute(1)
    rs1_send(1)
    compute(2)
    compute(3)
    rs1_agg(0)
    rs1_agg(1)
    rs1_send(2)
    rs1_send(3)
    rs1_fin(0)
    rs1_fin(1)
    rs1_agg(2)
    rs1_agg(3)
    middle(0)
    middle(1)
    rs1_fin(2)
    rs1_fin(3)
    ag2_send(0)
    ag2_send(1)
    middle(2)
    middle(3)
    ag2_fwd(0)
    ag2_fwd(1)
    ag2_send(2)
    ag2_send(3)
    ag2_fin(0)
    post(0)
    ag2_fin(1)
    post(1)
    ag2_fwd(2)
    ag2_fwd(3)
    ag2_fin(2)
    post(2)
    ag2_fin(3)
    post(3)

    e2 = [(2.0 * acc_e[n]).astype(BF16) for n in range(3)]
    acc_o[...] += nn(e2[2], dout[...])
    acc_i[...] += nn(e2[0], at[0]) + nn(e2[1], at[1])
    tail = (slice(0, DS), slice(DS, 2 * DS), slice(2 * DS, 2 * DS + EXT))

    def rows_of(xi, c):
        return pl.ds(pl.multiple_of((xi * 2 + c) * 32, 32), 32)

    def mine_rows(xi, c):
        r = rows_of(xi, c)
        e = jnp.concatenate(
            [acc_e[0, r], acc_e[1, r], acc_e[2, r], jnp.zeros((32, R), F32)], axis=1)
        return acc_o[r, :], acc_i[r, :], e

    for xi in range(X):
        for cols, v in zip(tail, mine_rows(xi, other)):
            qt[xi, :, cols] = v.astype(BF16)
    pair = put(qt, rt, {"c": other})
    pair.wait_recv()
    xr = []
    for off in (2, 1, 3):
        xi = at_off("x", off)
        for cols, v in zip(tail, mine_rows(xi, me["c"])):
            uq[off - 1, :, cols] = (v + rt[xi, :, cols].astype(F32)).astype(BF16)
        xr.append(put(uq.at[off - 1], rx.at[off - 1], {"x": xi}))
    grads()
    own = [v + rt[me["x"], :, cols].astype(F32) for cols, v in zip(tail, mine_rows(me["x"], me["c"]))]
    for c in xr:
        c.wait_recv()
    res = []
    for cols, v in zip(tail, own):
        for n in range(3):
            v = v + rx[n, :, cols].astype(F32)
        res.append(v.astype(BF16))
    eg[my_dp] = res[2]
    mine = eg.at[my_dp]
    er = [put(mine, mine, {"c": other})]
    for off in (2, 1, 3):
        er.append(put(mine, mine, {"x": at_off("x", off)}))
        er.append(put(mine, mine, {"x": at_off("x", off), "c": other}))
    o_out[...] = res[0]
    o_in[...] = res[1]
    for c in er:
        c.wait_recv()
    e_t = jnp.transpose(eg[...].reshape(T, EXT).astype(F32)).astype(BF16)
    for k in range(2):
        o_gl[k] = SCALE * nn(e_t[64 * k:64 * k + 64], xc[0].reshape(T, DS))
    o_do[...] = SCALE * nn(e_t[128:192], xc[1].reshape(T, DS))
    for c in started:
        c.wait_send()


def per_device(tok, w, wd, a, b, din, dout, cot):
    at = jnp.swapaxes(a, 1, 2)
    dint = jnp.swapaxes(din, 0, 1)
    vm = pltpu.VMEM
    scratch = [
        vm((2, X * C, 32, DS), BF16), vm((2, DS, FS), BF16), vm((FS, DS), BF16),
        vm((2, R, DS), BF16), vm((2, R, FS), BF16), vm((R, FS), BF16), vm((R, DS), BF16),
        vm((T, DS), F32), vm((T, DS), F32), vm((3, T, R), F32),
        vm((X, 32, 2 * DS + EXT), BF16), vm((X, 32, 2 * DS + EXT), BF16),
        vm((3, 32, 2 * DS + EXT), BF16), vm((3, 32, 2 * DS + EXT), BF16),
        vm((X * C, 32, EXT), BF16),
    ]
    for wid in WIDTHS:
        scratch += [
            vm((Y, Z, 16, wid), F32), vm((Y, Z, 16, wid), BF16),
            vm((2, 16, wid), BF16), vm((2, 16, wid), BF16),
            vm((2, 16, wid), BF16), vm((2, 16, wid), BF16),
            vm((4, 16, wid), BF16), vm((4, 16, wid), BF16),
            vm((4, 16, wid), F32), vm((4, 16, wid), BF16), vm((3, 16, wid), BF16),
            vm((Y, Z, 16, wid), BF16),
        ]
    scratch += [pltpu.SemaphoreType.DMA((8,)), pltpu.SemaphoreType.DMA((N_SEM,)), pltpu.SemaphoreType.DMA((N_SEM,))]
    anyspec = pl.BlockSpec(memory_space=pl.ANY)
    vspec = pl.BlockSpec(memory_space=pltpu.VMEM)
    out, inp, gl, gf, di, do = pl.pallas_call(
        body,
        out_shape=(
            jax.ShapeDtypeStruct((32, DS), BF16), jax.ShapeDtypeStruct((32, DS), BF16),
            jax.ShapeDtypeStruct((2, R, DS), F32), jax.ShapeDtypeStruct((2, R, FS), F32),
            jax.ShapeDtypeStruct((R, FS), F32), jax.ShapeDtypeStruct((R, DS), F32),
        ),
        in_specs=[anyspec] * 8,
        out_specs=(vspec,) * 6,
        scratch_shapes=scratch,
        compiler_params=pltpu.CompilerParams(
            collective_id=0, has_side_effects=True, vmem_limit_bytes=60 * 1024 * 1024),
        name="layer",
    )(tok, w, wd, at, b, dint, dout, cot)
    return out, inp, jnp.swapaxes(gl, 1, 2), gf, jnp.swapaxes(di, 0, 1), do


def solution(mesh):
    torus = Mesh(mesh.devices.reshape(X, C, Y, Z), ("x", "c", "y", "z"))
    dp, mp = ("x", "c"), ("y", "z")
    in_specs = (
        P(dp, mp), P(None, mp, dp), P(dp, mp), P(None, mp, None),
        P(None, None, dp), P(dp, None), P(None, mp), P(dp, mp),
    )
    out_specs = (P(dp, mp), P(dp, mp), P(None, mp, None), P(None, None, dp), P(dp, None), P(None, mp))
    return jax.shard_map(per_device, mesh=torus, in_specs=in_specs, out_specs=out_specs, check_vma=False)
```

time: 347 us -> 83.2 us (0.24)
  waiting for transfers between devices: 215 us -> 0 us
  Pallas kernels: 0 us -> 72.1 us
  starting transfers between devices: 34.3 us -> 0 us
  matrix products: 23.7 us -> 0 us
  blocking collectives: 22 us -> 0 us
  between operations: 16.1 us -> 0.65 us
  other arithmetic: 12 us -> 0 us
  local copies, waits for them, and re-layouts: 21.4 us -> 10 us
    psum x1 -> x0, waiting for transfers between devices: 79.5 us -> none  [per_device(): lax.psum(upper_partial, MP)]
    pallas_call x0 -> x1, Pallas kernels: none -> 72.1 us  [per_device(): pl.pallas_call(body, out_shape=(jax.ShapeDtypeStruct((32, DS), BF16), jax...]
    reduce_scatter x4 -> x0, waiting for transfers between devices: 47.6 us -> none  [sum_in_order(): parts = lax.psum_scatter(parts, axes[k], scatter_dimension=0, tiled=True)]
    unnamed x7 -> x0, waiting for transfers between devices: 45.6 us -> none
    all_to_all x6 -> x0, waiting for transfers between devices: 41.9 us -> none  [the longest x4 33.5 us: sent_to_all(): lax.all_to_all(jnp.broadcast_to(array[None], (length, *array.shape)), axi...]
    all_to_all x6 -> x0, starting transfers between devices: 34.1 us -> none  [the longest x4 19.9 us: sent_to_all(): lax.all_to_all(jnp.broadcast_to(array[None], (length, *array.shape)), axi...]
    dot_general x15 -> x0, matrix products: 23.4 us -> none  [the longest x1 4.71 us: per_device(): jnp.einsum('tkf,kdf->td', back_all, gate_up_weight, preferred_element_typ...]
    all_to_all x2 -> x0, blocking collectives: 22 us -> none  [sent_to_all(): lax.all_to_all(jnp.broadcast_to(array[None], (length, *array.shape)), axi...]
  transfers between devices with their start and end apart: 12 -> 0, of which waited for: 7 -> 0; matrix products, arithmetic and copies ran while one was open for 10% -> 0% of each run, Pallas kernels for 0% -> 0%
where the time goes in v1:
time: 83.2 us; the launch traced here: 82.8 us
  Pallas kernels  72.1 us (87%)
  local copies, waits for them, and re-layouts  10 us (12%)
    pallas_call x1, Pallas kernels, per_device(): pl.pallas_call(body, out_shape=(jax.ShapeDtypeStruct((32, DS), BF16), jax...  72.1 us
    unnamed x6, local copies, waits for them, and re-layouts  10 us

profile of v1, /device:TPU:1, one launch (start us, length us, event | category | flops | bytes accessed | tf_op | source)
XLA Modules:
  0.0 82.8 jit_solution(16897707629673143181)
XLA Ops:
  0.6 72.1 %layer.1 = (bf16[32,512]{1,0:T(8,128)(2,1)}, bf16[32,512]{1,0:T(8,128)(2,1)}, f32[2,64,512]{2,1,0:T(8,128)}, f32[2,64,1920]{2,1,0:T(8,128)}, f32[64,1920]{1,0:T(8,128)}, /*index=5*/f32[64,512]{1,0:T(8,128)}) custom-call(bf16[32,512]{1,0:T(8,128)(2,1)} %tok.1, bf16[2,512,1920]{2,1,0:T(8,128)(2,1)} %w_hbm.1, bf16[1920,512]{1,0:T(8,128)(2,1)} %wd_hbm.1, ...), custom_call_target="tpu_custom_call" | custom-call | tf_op jit(solution)/shard_map/layer/pallas_call | solution.py:396
  72.7 1.4 %copy.20 = bf16[32,512]{1,0:T(8,128)(2,1)} copy(bf16[32,512]{1,0:T(8,128)(2,1)} %get-tuple-element.24) | data formatting | bytes 65536
  74.1 1.4 %copy.21 = bf16[32,512]{1,0:T(8,128)(2,1)} copy(bf16[32,512]{1,0:T(8,128)(2,1)} %get-tuple-element.25) | data formatting | bytes 65536
  75.5 1.7 %copy.22 = f32[2,512,64]{1,2,0:T(8,128)} copy(f32[2,512,64]{1,2,0:T(8,128)} %bitcast.5) | data formatting | bytes 524288
  77.2 2.2 %copy.23 = f32[2,64,1920]{2,1,0:T(8,128)} copy(f32[2,64,1920]{2,1,0:T(8,128)} %get-tuple-element.27) | data formatting | bytes 1966080
  79.4 1.8 %copy.24 = f32[1920,64]{0,1:T(8,128)} copy(f32[1920,64]{0,1:T(8,128)} %bitcast.4) | data formatting | bytes 983040
  81.2 1.6 %copy.25 = f32[64,512]{1,0:T(8,128)} copy(f32[64,512]{1,0:T(8,128)} %get-tuple-element.29) | data formatting | bytes 262144

commit v2 on v1

v2 whole, which is shorter than its diff:
```python
import jax
import jax.numpy as jnp
from jax import lax
from jax.experimental import pallas as pl
from jax.experimental.pallas import tpu as pltpu
from jax.sharding import Mesh
from jax.sharding import PartitionSpec as P

MESH = pl.DeviceIdType.MESH
F32 = jnp.float32
BF16 = jnp.bfloat16

X, C, Y, Z = 4, 2, 4, 4
T = 256
DS = 512
FS = 1920
R = 64
EXT = 256
SCALE = 2.0 * T ** -0.5

SUBS = (
    ("z", 1024, 128, True), ("y", 0, 256, False), ("z", 1152, 256, False), ("y", 256, 256, False),
    ("z", 1408, 256, False), ("y", 512, 256, False), ("z", 1664, 256, False), ("y", 768, 256, False),
)
WIDTHS = tuple(3 * hw + (EXT if ext else 0) for _, _, hw, ext in SUBS)
NS = len(SUBS)
N_RECV = 11 + 8 * NS
N_SENT = 11 + NS


def steps_of(subs, *names):
    return [(name, s) for s in subs for name in names]


SCHEDULE = (
    steps_of(range(NS), "gu", "hb", "send")
    + steps_of(range(NS), "agg") + steps_of(range(NS), "sum") + steps_of(range(NS), "mid")
    + [("esend", 0)] + steps_of(range(4), "spread") + [("esum", 0)] + steps_of(range(4, NS), "spread")
    + steps_of(range(4), "fwd") + [("emore", 0)] + steps_of(range(4, NS), "fwd")
    + [("fin", 0), ("out", 0), ("in", 0), ("flip", 0), ("grad", 0)]
    + steps_of(range(1, 6), "fin", "out", "in", "grad") + [("efin", 0)]
    + steps_of((6,), "fin", "out", "in")
    + [("fin", 7), ("out", 7), ("pair", 0), ("in", 7), ("pair", 1), ("grad", 6), ("xsend", 0), ("xsend", 1),
       ("grad", 7), ("xfin", 0), ("xfin", 1)]
)


def nn(a, b):
    return jnp.dot(a, b, preferred_element_type=F32)


def nt(a, b):
    return lax.dot_general(a, b, (((1,), (1,)), ((), ())), preferred_element_type=F32)


def body(tok, w_hbm, wd_hbm, at_hbm, b_hbm, dint_hbm, dout_hbm, cot,
         o_out, o_in, o_gl, o_gf, o_di, o_do,
         xc, w, wd, aw, cw, ew, acc_o, acc_i, ext2, e_acc, ext_t, lora,
         qt, rt, uq, rx, e_out, e_in, e_n, eg, xn, bytes_ref, *rest):
    per = len(rest) - 3
    each = per // NS
    bufs = [rest[s * each:(s + 1) * each] for s in range(NS)]
    local_sem, send_sem, recv_sem = rest[per:]
    me = {a: lax.axis_index(a) for a in ("x", "c", "y", "z")}

    def at_off(axis, off):
        return lax.rem(me[axis] + off, 4)

    arrivals, departures = [], []

    def sends(like):
        departures.append(like)
        return len(departures) - 1

    def group(like, out=None):
        arrivals.append(like)
        return len(arrivals) - 1, sends(like) if out is None else out

    def put(g, src, dst, device):
        pltpu.make_async_remote_copy(
            src_ref=src, dst_ref=dst, send_sem=send_sem.at[g[1]], recv_sem=recv_sem.at[g[0]],
            device_id=device, device_id_type=MESH).start()

    def arrived(g):
        pltpu.make_async_copy(arrivals[g[0]], arrivals[g[0]], recv_sem.at[g[0]]).wait()

    def sent(n):
        pltpu.make_async_copy(departures[n], departures[n], send_sem.at[n]).wait()

    other = 1 - me["c"]
    barrier = pltpu.get_barrier_semaphore()
    partners = [{"c": other}]
    for off in (1, 2, 3):
        partners += [{"x": at_off("x", off)}, {"x": at_off("x", off), "c": other},
                     {"y": at_off("y", off)}, {"z": at_off("z", off)}]
    for p in partners:
        pl.semaphore_signal(barrier, inc=1, device_id=p, device_id_type=MESH)

    my_dp = me["x"] * 2 + me["c"]
    loads = []
    for n, (src, dst) in enumerate((
        (tok, xc.at[0, my_dp]), (cot, xc.at[1, my_dp]), (at_hbm, aw), (dout_hbm, cw.at[0:64]),
        (b_hbm.at[0], ew.at[0, 0:64]), (b_hbm.at[1], ew.at[1, 64:128]), (dint_hbm, ew.at[2, 0:64]),
        (w_hbm, w), (wd_hbm, wd),
    )):
        c = pltpu.make_async_copy(src, dst, local_sem.at[n])
        c.start()
        loads.append(c)
    cw[64:128, :] = jnp.zeros((64, DS), BF16)
    ew[0, 64:128, :] = jnp.zeros((64, FS), BF16)
    ew[1, 0:64, :] = jnp.zeros((64, FS), BF16)
    ew[2, 64:128, :] = jnp.zeros((64, FS), BF16)
    loads[0].wait()
    loads[1].wait()
    pl.semaphore_wait(barrier, len(partners))

    def block(n, off):
        return xc.at[n, at_off("x", off) * 2 + me["c"]]

    along = [group(xn.at[0:3]) for _ in range(2)]
    across = [group(xn) for _ in range(2)]
    for n in range(2):
        for off in (2, 1, 3):
            put(along[n], block(n, 0), block(n, 0), {"x": at_off("x", off)})
        put(across[n], block(n, 0), block(n, 0), {"c": other})
    for c in loads[2:]:
        c.wait()
    for n in range(2):
        arrived(along[n])
        for off in (1, 2, 3):
            put(across[n], block(n, off), block(n, off), {"c": other})

    arrived(across[0])
    xs = xc[0].reshape(T, DS)
    late = {}

    def seg(n, hw):
        return slice(n * hw, (n + 1) * hw)

    def keep(s, cols, v):
        v = v.reshape(Y, Z, 16, v.shape[-1])
        bufs[s][0][:, :, :, cols] = v
        bufs[s][1][:, :, :, cols] = v.astype(BF16)

    def compute_gu(s):
        _, f0, hw, _ = SUBS[s]
        cols = slice(f0, f0 + hw)
        for n in range(2):
            keep(s, seg(n, hw), nn(xs, w[n, :, cols]))

    def compute_hb(s):
        _, f0, hw, ext = SUBS[s]
        cols = slice(f0, f0 + hw)
        if not late:
            arrived(across[1])
            late["c"] = xc[1].reshape(T, DS)
        keep(s, seg(2, hw), nt(late["c"], wd[cols, :]))
        if ext:
            keep(s, slice(3 * hw, 3 * hw + 128), nt(xs, aw[...]))
            keep(s, slice(3 * hw + 128, 3 * hw + EXT), nt(late["c"], cw[...]))

    other_axis = {"y": "z", "z": "y"}

    def part(ref, s, a1, lo, hi):
        if SUBS[s][0] == "y":
            return ref.at[a1, lo:hi]
        return ref.at[lo:hi, a1]

    def value(ref, s, a1, a2):
        if SUBS[s][0] == "y":
            return ref[a1, a2]
        return ref[a2, a1]

    st = []
    for s in range(NS):
        tt, ff, r2 = bufs[s][2], bufs[s][4], bufs[s][7]
        o = sends(bytes_ref.at[:, :, 0:WIDTHS[s]])
        st.append({
            "t0": group(tt.at[0], o), "t1": group(tt.at[1], o), "f": group(ff, o), "r": group(r2, o),
            "a": group(r2, o), "b0": group(tt.at[0], o), "b1": group(tt.at[1], o), "b2": group(ff, o)})

    def ring(s):
        a = SUBS[s][0]
        return a, {a: at_off(a, 3)}, {a: at_off(a, 1)}

    def rs1_send(s):
        a, left, right = ring(s)
        q, tt, ff = bufs[s][1], bufs[s][2], bufs[s][4]
        put(st[s]["t0"], part(q, s, at_off(a, 2), 0, 2), tt.at[0], left)
        put(st[s]["t1"], part(q, s, at_off(a, 2), 2, 4), tt.at[1], right)
        put(st[s]["f"], part(q, s, at_off(a, 3), 2, 4), ff.at[0, 2:4], left)
        put(st[s]["f"], part(q, s, at_off(a, 1), 0, 2), ff.at[1, 0:2], right)

    def rs1_agg(s):
        a, left, right = ring(s)
        p, tt, gg, ff = bufs[s][0], bufs[s][2], bufs[s][3], bufs[s][4]
        arrived(st[s]["t0"])
        for j in range(2):
            gg[0, j] = (value(p, s, at_off(a, 3), j) + tt[0, j].astype(F32)).astype(BF16)
        put(st[s]["f"], gg.at[0], ff.at[0, 0:2], left)
        arrived(st[s]["t1"])
        for j in range(2):
            gg[1, j] = (value(p, s, at_off(a, 1), 2 + j) + tt[1, j].astype(F32)).astype(BF16)
        put(st[s]["f"], gg.at[1], ff.at[1, 2:4], right)

    def rs1_fin(s):
        a = SUBS[s][0]
        b = other_axis[a]
        p, ff, sm, q2, r2 = (bufs[s][k] for k in (0, 4, 5, 6, 7))
        arrived(st[s]["f"])
        for j in range(4):
            v = value(p, s, me[a], j) + ff[0, j].astype(F32) + ff[1, j].astype(F32)
            sm[j] = v
            q2[j] = v.astype(BF16)
        for off in (2, 1, 3):
            put(st[s]["r"], q2.at[at_off(b, off)], r2.at[off - 1], {b: at_off(b, off)})

    seen = set()

    def add(ref, key, v):
        if key in seen:
            v = v + ref[...]
        seen.add(key)
        ref[...] = v

    def middle(s):
        a, f0, hw, ext = SUBS[s]
        b = other_axis[a]
        sm, r2, act = (bufs[s][k] for k in (5, 7, 8))
        arrived(st[s]["r"])

        def total(cols):
            v = sm[me[b], :, cols]
            for n in range(3):
                v = v + r2[n, :, cols].astype(F32)
            return v

        my = (me["y"], me["z"])
        cols = slice(f0, f0 + hw)
        if ext:
            v = total(slice(3 * hw, 3 * hw + EXT)).astype(BF16)
            act[my[0], my[1], :, 3 * hw:] = v
            ext2[...] = 2.0 * v
        lows = (ext2[:, 0:128], ext2[:, 0:128], ext2[:, 128:256])
        gate, up, hb = (total(seg(n, hw)) + nn(lows[n], ew[n, :, cols]) for n in range(3))
        sg = 1.0 / (1.0 + jnp.exp(-gate))
        gs = gate * sg
        hid = (gs * up).astype(BF16)
        gb = (hb * up * sg * (1.0 + gate * (1.0 - sg))).astype(BF16)
        ub = (hb * gs).astype(BF16)
        act[my[0], my[1], :, seg(0, hw)] = hid
        act[my[0], my[1], :, seg(1, hw)] = gb
        act[my[0], my[1], :, seg(2, hw)] = ub
        mine = act.at[my[0], my[1]]
        for off in (2, 1, 3):
            put(st[s]["a"], mine, mine, {b: at_off(b, off)})
        add(e_acc.at[:, 0:128], "bl", nt(gb, ew[0, :, cols]) + nt(ub, ew[1, :, cols]))
        add(e_acc.at[:, 128:256], "ld", nt(hid, ew[2, :, cols]))

    def ag2_send(s):
        a, left, right = ring(s)
        act = bufs[s][8]
        arrived(st[s]["a"])
        lo, hi = part(act, s, me[a], 0, 2), part(act, s, me[a], 2, 4)
        put(st[s]["b0"], lo, lo, left)
        put(st[s]["b1"], hi, hi, right)
        put(st[s]["b2"], hi, hi, left)
        put(st[s]["b2"], lo, lo, right)

    def ag2_fwd(s):
        a, left, right = ring(s)
        act = bufs[s][8]
        arrived(st[s]["b0"])
        src = part(act, s, at_off(a, 1), 0, 2)
        put(st[s]["b2"], src, src, left)
        arrived(st[s]["b1"])
        src = part(act, s, at_off(a, 3), 2, 4)
        put(st[s]["b2"], src, src, right)

    def ag2_fin(s):
        arrived(st[s]["b2"])

    def act_of(s, cols):
        return bufs[s][8][:, :, :, cols].reshape(T, cols.stop - cols.start)

    def post_o(s):
        _, f0, hw, _ = SUBS[s]
        add(acc_o, "o", nn(act_of(s, seg(0, hw)), wd[f0:f0 + hw, :]))

    def post_i(s):
        _, f0, hw, _ = SUBS[s]
        cols = slice(f0, f0 + hw)
        add(acc_i, "i", nt(act_of(s, seg(1, hw)), w[0, :, cols]) + nt(act_of(s, seg(2, hw)), w[1, :, cols]))

    def flip(_):
        hw = SUBS[0][2]
        ext = act_of(0, slice(3 * hw, 3 * hw + EXT)).astype(F32)
        ext_t[...] = jnp.transpose(ext).astype(BF16)

    def grads(s):
        _, f0, hw, _ = SUBS[s]
        cols = slice(f0, f0 + hw)
        for k in range(2):
            o_gf[k, :, cols] = SCALE * nn(ext_t[64 * k:64 * k + 64, :], act_of(s, seg(1 + k, hw)))
        o_di[:, cols] = SCALE * nn(ext_t[128:192, :], act_of(s, seg(0, hw)))

    my_rows = (me["y"], me["z"])
    e_dp, e_z, e_y = group(e_in), group(e_n.at[0]), group(e_n)
    hops = [(off, d) for off in (2, 1, 3, 0) for d in (0, 1) if off or d]

    def e_send(_):
        e_out[...] = e_acc[...].astype(BF16)
        for n, (off, d) in enumerate(hops):
            put(e_dp, e_out, e_in.at[n], {"x": at_off("x", off), "c": lax.rem(me["c"] + d, 2)})

    def e_sum(_):
        arrived(e_dp)
        v = e_acc[...]
        for n in range(7):
            v = v + e_in[n].astype(F32)
        eg[my_rows[0], my_rows[1]] = v.astype(BF16)
        mine = eg.at[my_rows[0], my_rows[1]]
        for off in (2, 1, 3):
            put(e_z, mine, mine, {"z": at_off("z", off)})

    def e_more(_):
        arrived(e_z)
        mine = eg.at[my_rows[0]]
        for off in (2, 1, 3):
            put(e_y, mine, mine, {"y": at_off("y", off)})

    def e_fin(_):
        arrived(e_y)
        e_t = jnp.transpose(eg[...].reshape(T, EXT).astype(F32)).astype(BF16)
        for k in range(2):
            o_gl[k] = SCALE * nn(e_t[64 * k:64 * k + 64], xc[0].reshape(T, DS))
        o_do[...] = SCALE * nn(e_t[128:192], xc[1].reshape(T, DS))
        e2 = 2.0 * eg[me["x"], pl.ds(2 * me["c"], 2)].reshape(32, EXT)
        lora[0] = nn(e2[:, 128:256], cw[...])
        lora[1] = nn(e2[:, 0:128], aw[...])

    pair = [group(qt.at[n]) for n in range(2)]
    b_x = [group(rx.at[n]) for n in range(2)]
    accs, res = (acc_o, acc_i), (o_out, o_in)

    def rows_of(xi, c):
        return pl.ds(pl.multiple_of((xi * 2 + c) * 32, 32), 32)

    def pair_send(n):
        for xi in range(X):
            qt[n, xi] = accs[n][rows_of(xi, other), :].astype(BF16)
        put(pair[n], qt.at[n], rt.at[n], {"c": other})

    def x_send(n):
        arrived(pair[n])
        for off in (2, 1, 3):
            xi = at_off("x", off)
            v = accs[n][rows_of(xi, me["c"]), :] + rt[n, xi].astype(F32)
            uq[n, off - 1] = v.astype(BF16)
            put(b_x[n], uq.at[n, off - 1], rx.at[n, off - 1], {"x": xi})

    def x_fin(n):
        v = accs[n][rows_of(me["x"], me["c"]), :] + rt[n, me["x"]].astype(F32) + lora[n]
        arrived(b_x[n])
        for k in range(3):
            v = v + rx[n, k].astype(F32)
        res[n][...] = v.astype(BF16)

    steps = {"gu": compute_gu, "hb": compute_hb, "send": rs1_send, "agg": rs1_agg, "sum": rs1_fin,
             "mid": middle, "spread": ag2_send, "fwd": ag2_fwd, "fin": ag2_fin,
             "out": post_o, "in": post_i, "flip": flip, "grad": grads,
             "esend": e_send, "esum": e_sum, "emore": e_more, "efin": e_fin,
             "pair": pair_send, "xsend": x_send, "xfin": x_fin}
    for step, s in SCHEDULE:
        with jax.named_scope(step + str(s)):
            steps[step](s)
    for n in range(len(departures)):
        sent(n)
    assert (len(arrivals), len(departures)) == (N_RECV, N_SENT), (len(arrivals), len(departures))


RESULTS = (
    ((32, DS), BF16), ((32, DS), BF16), ((2, R, DS), F32),
    ((2, R, FS), F32), ((R, FS), F32), ((R, DS), F32),
)


def store(*refs):
    copies = [pltpu.make_async_copy(refs[n], refs[6 + n], refs[12].at[n]) for n in (3, 4, 2, 5, 0, 1)]
    for c in copies:
        c.start()
    for c in copies:
        c.wait()


def per_device(tok, w, wd, a, b, din, dout, cot):
    at = jnp.swapaxes(a, 1, 2).reshape(2 * R, DS)
    dint = jnp.swapaxes(din, 0, 1)
    vm = pltpu.VMEM
    scratch = [
        vm((2, X * C, 32, DS), BF16), vm((2, DS, FS), BF16), vm((FS, DS), BF16),
        vm((128, DS), BF16), vm((128, DS), BF16), vm((3, 128, FS), BF16),
        vm((T, DS), F32), vm((T, DS), F32),
        vm((16, EXT), BF16), vm((16, EXT), F32), vm((EXT, T), BF16), vm((2, 32, DS), F32),
        vm((2, X, 32, DS), BF16), vm((2, X, 32, DS), BF16),
        vm((2, 3, 32, DS), BF16), vm((2, 3, 32, DS), BF16),
        vm((16, EXT), BF16), vm((7, 16, EXT), BF16), vm((4, 3, 16, EXT), BF16), vm((Y, Z, 16, EXT), BF16),
        vm((4, 32, DS), BF16), vm((30, 16, max(WIDTHS)), BF16),
    ]
    for wid in WIDTHS:
        scratch += [
            vm((Y, Z, 16, wid), F32), vm((Y, Z, 16, wid), BF16),
            vm((2, 2, 16, wid), BF16), vm((2, 2, 16, wid), BF16), vm((2, 4, 16, wid), BF16),
            vm((4, 16, wid), F32), vm((4, 16, wid), BF16), vm((3, 16, wid), BF16),
            vm((Y, Z, 16, wid), BF16),
        ]
    scratch += [pltpu.SemaphoreType.DMA((9,)), pltpu.SemaphoreType.DMA((N_SENT,)), pltpu.SemaphoreType.DMA((N_RECV,))]
    anyspec = pl.BlockSpec(memory_space=pltpu.MemorySpace.HBM)
    vspec = pl.BlockSpec(memory_space=pltpu.VMEM)
    res = pl.pallas_call(
        body,
        out_shape=tuple(vm(s, d) for s, d in RESULTS),
        in_specs=[anyspec] * 8,
        out_specs=(vspec,) * 6,
        scratch_shapes=scratch,
        compiler_params=pltpu.CompilerParams(
            collective_id=0, has_side_effects=True, vmem_limit_bytes=40 * 1024 * 1024),
        name="layer",
    )(*(pltpu.with_memory_space_constraint(v, pltpu.MemorySpace.HBM)
        for v in (tok, w, wd, at, b, dint, dout, cot)))
    out, inp, gl, gf, di, do = pl.pallas_call(
        store,
        out_shape=tuple(jax.ShapeDtypeStruct(s, d) for s, d in RESULTS),
        in_specs=[vspec] * 6,
        out_specs=(anyspec,) * 6,
        scratch_shapes=[pltpu.SemaphoreType.DMA((6,))],
        compiler_params=pltpu.CompilerParams(vmem_limit_bytes=1024 * 1024),
        name="store",
    )(*res)
    return out, inp, jnp.swapaxes(gl, 1, 2), gf, jnp.swapaxes(di, 0, 1), do


def solution(mesh):
    torus = Mesh(mesh.devices.reshape(X, C, Y, Z), ("x", "c", "y", "z"))
    dp, mp = ("x", "c"), ("y", "z")
    in_specs = (
        P(dp, mp), P(None, mp, dp), P(dp, mp), P(None, mp, None),
        P(None, None, dp), P(dp, None), P(None, mp), P(dp, mp),
    )
    out_specs = (P(dp, mp), P(dp, mp), P(None, mp, None), P(None, None, dp), P(dp, None), P(None, mp))
    return jax.shard_map(per_device, mesh=torus, in_specs=in_specs, out_specs=out_specs, check_vma=False)
```

time: 83.2 us -> 61.7 us (0.74)
  Pallas kernels: 72.1 us -> 60.9 us
  local copies, waits for them, and re-layouts: 10 us -> 0 us
    pallas_call x1 -> x2, Pallas kernels: 72.1 us -> 60.9 us  [the longest x1 59.6 us: per_device(): pl.pallas_call(body, out_shape=tuple((vm(s, d) for s, d in RESULTS)), in_...]
    unnamed x6 -> x0, local copies, waits for them, and re-layouts: 10 us -> none
where the time goes in v2:
time: 61.7 us; the launch traced here: 61.6 us
  Pallas kernels  60.9 us (99%)
  between operations  0.64 us (1%)
    pallas_call x1, Pallas kernels, per_device(): pl.pallas_call(body, out_shape=tuple((vm(s, d) for s, d in RESULTS)), in_...  59.6 us
    pallas_call x1, Pallas kernels, per_device(): pl.pallas_call(store, out_shape=tuple((jax.ShapeDtypeStruct(s, d) for s,...  1.3 us

profile of v2, /device:TPU:1, one launch (start us, length us, event | category | flops | bytes accessed | tf_op | source)
XLA Modules:
  0.0 61.6 jit_solution(15049678484929300010)
XLA Ops:
  0.6 59.6 %layer.1 = (bf16[32,512]{1,0:T(8,128)(2,1)S(1)}, bf16[32,512]{1,0:T(8,128)(2,1)S(1)}, f32[2,64,512]{2,1,0:T(8,128)S(1)}, f32[2,64,1920]{2,1,0:T(8,128)S(1)}, f32...) custom-call(bf16[32,512]{1,0:T(8,128)(2,1)} %tok.1, bf16[2,512,1920]{2,1,0:T(8,128)(2,1)} %w_hbm.1, bf16[1920,512]{1,0:T(8,128)(2,1)} %wd_hbm.1, ...), custom_call_target="tpu_custom_call" | custom-call | tf_op jit(solution)/shard_map/layer/pallas_call | solution.py:420
  60.3 1.3 %store.1 = (bf16[32,512]{1,0:T(8,128)(2,1)}, bf16[32,512]{1,0:T(8,128)(2,1)}, f32[2,64,512]{2,1,0:T(8,128)}, f32[2,64,1920]{2,1,0:T(8,128)}, f32[64,1920]{1,0:T(8,128)}, /*index=5*/f32[64,512]{1,0:T(8,128)}) custom-call(bf16[32,512]{1,0:T(8,128)(2,1)S(1)} %get-tuple-element.18.refs_0_, bf16[32,512]{1,0:T(8,128)(2,1)S(1)} %get-tuple-element.19.refs_1_, ...), custom_call_target="tpu_custom_call" | custom-call | tf_op jit(solution)/shard_map/store/pallas_call | solution.py:431

commit v3 on v2

v3 whole, which is shorter than its diff:
```python
import math

import jax
import jax.numpy as jnp
from jax import lax
from jax.experimental import pallas as pl
from jax.experimental.pallas import tpu as pltpu
from jax.sharding import Mesh
from jax.sharding import PartitionSpec as P

MESH = pl.DeviceIdType.MESH
F32 = jnp.float32
BF16 = jnp.bfloat16

X, C, Y, Z = 4, 2, 4, 4
T = 256
DS = 512
FS = 1920
R = 64
EXT = 256
SCALE = 2.0 * T ** -0.5

SUBS = (
    ("z", 1024, 128, True), ("y", 0, 256, False), ("z", 1152, 256, False), ("y", 256, 256, False),
    ("z", 1408, 256, False), ("y", 512, 256, False), ("z", 1664, 256, False), ("y", 768, 256, False),
)
WIDTHS = tuple(3 * hw + (EXT if ext else 0) for _, _, hw, ext in SUBS)
HALVES = {"y": (0, 1024, 1024), "z": (1024, 896, 896 + EXT)}
NS = len(SUBS)
N_RECV = 17 + 6 * NS
TILE = 16 * 128
SENT_TILES = 30 * sum(WIDTHS) // 128 + 268
LOAD_TILES = (3 * R * DS + 3 * R * FS + 3 * DS * FS) // TILE


def steps_of(subs, *names):
    return [(name, s) for s in subs for name in names]


SCHEDULE = (
    steps_of(range(3), "gu", "sendgu") + steps_of(range(3), "hb", "sendhb")
    + steps_of(range(3, NS), "gu", "sendgu", "hb", "sendhb")
    + steps_of(range(NS), "agg") + steps_of(range(NS), "sum") + steps_of(range(NS), "mid", "near")
    + [("esend", 0)] + steps_of(range(4), "spread") + steps_of(range(2), "hspread") + steps_of(range(4, 6), "spread")
    + steps_of(range(2), "hfwd") + steps_of(range(6, NS), "spread") + steps_of(range(4), "fwd")
    + [("esum", 0)] + steps_of(range(4, 6), "fwd")
    + [("hfin", 0), ("hfin", 1), ("out", 0), ("pair", 0)]
    + steps_of(range(6, NS), "fwd") + steps_of(range(2), "fin", "in") + [("xsend", 0)]
    + steps_of(range(2, 4), "fin", "in") + [("emore", 0)]
    + steps_of(range(4, NS), "fin", "in") + [("pair", 1), ("flip", 0), ("hgrad", 0)]
    + steps_of(range(3), "grad") + [("xsend", 1)] + steps_of(range(3, NS), "grad")
    + [("efin", 0), ("xfin", 0), ("xfin", 1)]
)


def nn(a, b):
    return jnp.dot(a, b, preferred_element_type=F32)


def nt(a, b):
    return lax.dot_general(a, b, (((1,), (1,)), ((), ())), preferred_element_type=F32)


def body(tok, w_hbm, wd_hbm, at_hbm, b_hbm, dint_hbm, dout_hbm, cot,
         o_out, o_in, o_gl, o_gf, o_di, o_do,
         xc, w, wd, aw, cw, ew, acc_o, acc_i, ext2, e_acc, ext_t, lora,
         qt, rt, uq, rx, e_out, e_in, eg, bytes_ref, h_y, h_z, *rest):
    per = len(rest) - 3
    each = per // NS
    bufs = [rest[s * each:(s + 1) * each] for s in range(NS)]
    local_sem, send_sem, recv_sem = rest[per:]
    me = {a: lax.axis_index(a) for a in ("x", "c", "y", "z")}

    def at_off(axis, off):
        return lax.rem(me[axis] + off, 4)

    arrivals, moved = [], [0]

    def bytes_of(tiles):
        return bytes_ref.at[0:tiles]

    def group(like):
        arrivals.append(like)
        return len(arrivals) - 1

    def put(g, src, dst, device):
        moved[0] += math.prod(src.shape) // TILE
        pltpu.make_async_remote_copy(
            src_ref=src, dst_ref=dst, send_sem=send_sem, recv_sem=recv_sem.at[g],
            device_id=device, device_id_type=MESH).start()

    def arrived(g):
        size = bytes_of(arrivals[g])
        pltpu.make_async_copy(size, size, recv_sem.at[g]).wait()

    other = 1 - me["c"]
    barrier = pltpu.get_barrier_semaphore()
    partners = [{"c": other}]
    for off in (1, 2, 3):
        partners += [{"x": at_off("x", off)}, {"x": at_off("x", off), "c": other},
                     {"y": at_off("y", off)}, {"z": at_off("z", off)}]
    for p in partners:
        pl.semaphore_signal(barrier, inc=1, device_id=p, device_id_type=MESH)

    my_dp = me["x"] * 2 + me["c"]
    loads = []
    for n, (src, dst) in enumerate(((tok, xc.at[0, my_dp]), (cot, xc.at[1, my_dp]))):
        loads.append(pltpu.make_async_copy(src, dst, local_sem.at[n]))
        loads[n].start()
    for src, dst in (
        (at_hbm, aw), (dout_hbm, cw.at[0:64]), (b_hbm.at[0], ew.at[0, 0:64]), (b_hbm.at[1], ew.at[1, 64:128]),
        (dint_hbm, ew.at[2, 0:64]), (w_hbm, w), (wd_hbm, wd),
    ):
        pltpu.make_async_copy(src, dst, local_sem.at[2]).start()
    cw[64:128, :] = jnp.zeros((64, DS), BF16)
    ew[0, 64:128, :] = jnp.zeros((64, FS), BF16)
    ew[1, 0:64, :] = jnp.zeros((64, FS), BF16)
    ew[2, 64:128, :] = jnp.zeros((64, FS), BF16)
    loads[0].wait()
    loads[1].wait()
    pl.semaphore_wait(barrier, len(partners))

    def block(n, off):
        return xc.at[n, at_off("x", off) * 2 + me["c"]]

    along = [group(3 * 8) for _ in range(2)]
    across = [group(4 * 8) for _ in range(2)]
    for n in range(2):
        for off in (2, 1, 3):
            put(along[n], block(n, 0), block(n, 0), {"x": at_off("x", off)})
        put(across[n], block(n, 0), block(n, 0), {"c": other})
    pltpu.make_async_copy(bytes_of(LOAD_TILES), bytes_of(LOAD_TILES), local_sem.at[2]).wait()
    for n in range(2):
        arrived(along[n])
        for off in (1, 2, 3):
            put(across[n], block(n, off), block(n, off), {"c": other})

    arrived(across[0])
    seen = set()

    def rows_all(n):
        return xc[n].reshape(T, DS)

    def seg(n, hw):
        return slice(n * hw, (n + 1) * hw)

    def keep(s, cols, v):
        v = v.reshape(Y, Z, 16, v.shape[-1])
        bufs[s][0][:, :, :, cols] = v
        bufs[s][1][:, :, :, cols] = v.astype(BF16)

    def compute_gu(s):
        _, f0, hw, _ = SUBS[s]
        cols = slice(f0, f0 + hw)
        for n in range(2):
            keep(s, seg(n, hw), nn(rows_all(0), w[n, :, cols]))

    def compute_hb(s):
        _, f0, hw, ext = SUBS[s]
        cols = slice(f0, f0 + hw)
        if "cot" not in seen:
            arrived(across[1])
            seen.add("cot")
        keep(s, seg(2, hw), nt(rows_all(1), wd[cols, :]))
        if ext:
            keep(s, slice(3 * hw, 3 * hw + 128), nt(rows_all(0), aw[...]))
            keep(s, slice(3 * hw + 128, 3 * hw + EXT), nt(rows_all(1), cw[...]))

    other_axis = {"y": "z", "z": "y"}

    def part(ref, a, a1, lo, hi, cols=slice(None)):
        if a == "y":
            return ref.at[a1, lo:hi, :, cols]
        return ref.at[lo:hi, a1, :, cols]

    def value(ref, s, a1, a2):
        if SUBS[s][0] == "y":
            return ref[a1, a2]
        return ref[a2, a1]

    st = []
    for s in range(NS):
        n, g = WIDTHS[s] // 128, 2 * SUBS[s][2] // 128
        st.append({"t": group(4 * n), "f": group(8 * n), "r": group(3 * n),
                   "a": group(3 * g), "t2": group(4 * g), "b": group(8 * g)})

    halves = {"y": h_y, "z": h_z}
    hst = {}
    for a, (_, _, n) in HALVES.items():
        hst[a] = {"a": group(3 * n // 128), "t2": group(4 * n // 128), "b": group(8 * n // 128)}

    def ring(s):
        a = SUBS[s][0]
        return a, {a: at_off(a, 3)}, {a: at_off(a, 1)}

    def rs1_send(s, cols):
        a, left, right = ring(s)
        q, tt, ff = bufs[s][1], bufs[s][2], bufs[s][4]
        put(st[s]["t"], part(q, a, at_off(a, 2), 0, 2, cols), tt.at[0, :, :, cols], left)
        put(st[s]["t"], part(q, a, at_off(a, 2), 2, 4, cols), tt.at[1, :, :, cols], right)
        put(st[s]["f"], part(q, a, at_off(a, 3), 2, 4, cols), ff.at[0, 2:4, :, cols], left)
        put(st[s]["f"], part(q, a, at_off(a, 1), 0, 2, cols), ff.at[1, 0:2, :, cols], right)

    def rs1_agg(s):
        a, left, right = ring(s)
        p, tt, gg, ff = bufs[s][0], bufs[s][2], bufs[s][3], bufs[s][4]
        arrived(st[s]["t"])
        for j in range(2):
            gg[0, j] = (value(p, s, at_off(a, 3), j) + tt[0, j].astype(F32)).astype(BF16)
        put(st[s]["f"], gg.at[0], ff.at[0, 0:2], left)
        for j in range(2):
            gg[1, j] = (value(p, s, at_off(a, 1), 2 + j) + tt[1, j].astype(F32)).astype(BF16)
        put(st[s]["f"], gg.at[1], ff.at[1, 2:4], right)

    def rs1_fin(s):
        a = SUBS[s][0]
        b = other_axis[a]
        p, ff, sm, q2, r2 = (bufs[s][k] for k in (0, 4, 5, 6, 7))
        arrived(st[s]["f"])
        for j in range(4):
            v = value(p, s, me[a], j) + ff[0, j].astype(F32) + ff[1, j].astype(F32)
            sm[j] = v
            q2[j] = v.astype(BF16)
        for off in (2, 1, 3):
            put(st[s]["r"], q2.at[at_off(b, off)], r2.at[off - 1], {b: at_off(b, off)})

    def add(ref, key, v):
        if key in seen:
            v = v + ref[...]
        seen.add(key)
        ref[...] = v

    def middle(s):
        a, f0, hw, ext = SUBS[s]
        b = other_axis[a]
        sm, r2, act = (bufs[s][k] for k in (5, 7, 8))
        hid_ref, h0 = halves[a], f0 - HALVES[a][0]
        arrived(st[s]["r"])

        def total(cols):
            v = sm[me[b], :, cols]
            for n in range(3):
                v = v + r2[n, :, cols].astype(F32)
            return v

        my = (me["y"], me["z"])
        cols = slice(f0, f0 + hw)
        if ext:
            v = total(slice(3 * hw, 3 * hw + EXT)).astype(BF16)
            hid_ref[my[0], my[1], :, HALVES[a][1]:] = v
            ext2[...] = 2.0 * v
        lows = (ext2[:, 0:128], ext2[:, 0:128], ext2[:, 128:256])
        gate, up, hb = (total(seg(n, hw)) + nn(lows[n], ew[n, :, cols]) for n in range(3))
        sg = 1.0 / (1.0 + jnp.exp(-gate))
        gs = gate * sg
        hid = (gs * up).astype(BF16)
        gb = (hb * up * sg * (1.0 + gate * (1.0 - sg))).astype(BF16)
        ub = (hb * gs).astype(BF16)
        hid_ref[my[0], my[1], :, h0:h0 + hw] = hid
        act[my[0], my[1], :, seg(0, hw)] = gb
        act[my[0], my[1], :, seg(1, hw)] = ub
        pieces = [slice(h0, h0 + hw)] + ([slice(HALVES[a][1], HALVES[a][1] + EXT)] if ext else [])
        for piece in pieces:
            mine = hid_ref.at[my[0], my[1], :, piece]
            for off in (2, 1, 3):
                put(hst[a]["a"], mine, mine, {b: at_off(b, off)})
        add(e_acc.at[:, 0:128], "bl", nt(gb, ew[0, :, cols]) + nt(ub, ew[1, :, cols]))
        add(e_acc.at[:, 128:256], "ld", nt(hid, ew[2, :, cols]))

    def near(s):
        b = other_axis[SUBS[s][0]]
        mine = bufs[s][8].at[me["y"], me["z"]]
        for off in (2, 1, 3):
            put(st[s]["a"], mine, mine, {b: at_off(b, off)})

    def spread(ref, a, groups):
        left, right = {a: at_off(a, 3)}, {a: at_off(a, 1)}
        arrived(groups["a"])
        lo, hi = part(ref, a, me[a], 0, 2), part(ref, a, me[a], 2, 4)
        put(groups["t2"], lo, lo, left)
        put(groups["t2"], hi, hi, right)
        put(groups["b"], hi, hi, left)
        put(groups["b"], lo, lo, right)

    def forward(ref, a, groups):
        left, right = {a: at_off(a, 3)}, {a: at_off(a, 1)}
        arrived(groups["t2"])
        src = part(ref, a, at_off(a, 1), 0, 2)
        put(groups["b"], src, src, left)
        src = part(ref, a, at_off(a, 3), 2, 4)
        put(groups["b"], src, src, right)

    def all_rows(ref, cols):
        return ref[:, :, :, cols].reshape(T, cols.stop - cols.start)

    def post_o(_):
        v = [nn(all_rows(halves[a], slice(0, n)), wd[f0:f0 + n, :]) for a, (f0, n, _) in HALVES.items()]
        acc_o[...] = v[0] + v[1]

    def post_i(s):
        _, f0, hw, _ = SUBS[s]
        cols = slice(f0, f0 + hw)
        act = bufs[s][8]
        add(acc_i, "i", nt(all_rows(act, seg(0, hw)), w[0, :, cols]) + nt(all_rows(act, seg(1, hw)), w[1, :, cols]))

    def flip(_):
        n = HALVES["z"][1]
        ext_t[...] = jnp.transpose(all_rows(h_z, slice(n, n + EXT)).astype(F32)).astype(BF16)

    def h_grads(_):
        for a, (f0, n, _) in HALVES.items():
            o_di[:, f0:f0 + n] = SCALE * nn(ext_t[128:192, :], all_rows(halves[a], slice(0, n)))

    def grads(s):
        _, f0, hw, _ = SUBS[s]
        cols = slice(f0, f0 + hw)
        for k in range(2):
            o_gf[k, :, cols] = SCALE * nn(ext_t[64 * k:64 * k + 64, :], all_rows(bufs[s][8], seg(k, hw)))

    my_rows = (me["y"], me["z"])
    e_dp, e_z, e_y = group(7 * 2), group(3 * 2), group(12 * 2)
    hops = [(off, d) for off in (2, 1, 3, 0) for d in (0, 1) if off or d]

    def e_send(_):
        e_out[...] = e_acc[...].astype(BF16)
        for n, (off, d) in enumerate(hops):
            put(e_dp, e_out, e_in.at[n], {"x": at_off("x", off), "c": lax.rem(me["c"] + d, 2)})

    def e_sum(_):
        arrived(e_dp)
        v = e_acc[...]
        for n in range(7):
            v = v + e_in[n].astype(F32)
        eg[my_rows[0], my_rows[1]] = v.astype(BF16)
        mine = eg.at[my_rows[0], my_rows[1]]
        for off in (2, 1, 3):
            put(e_z, mine, mine, {"z": at_off("z", off)})

    def e_more(_):
        arrived(e_z)
        mine = eg.at[my_rows[0]]
        for off in (2, 1, 3):
            put(e_y, mine, mine, {"y": at_off("y", off)})

    def e_fin(_):
        arrived(e_y)
        e_t = jnp.transpose(eg[...].reshape(T, EXT).astype(F32)).astype(BF16)
        for k in range(2):
            o_gl[k] = SCALE * nn(e_t[64 * k:64 * k + 64], xc[0].reshape(T, DS))
        o_do[...] = SCALE * nn(e_t[128:192], xc[1].reshape(T, DS))
        e2 = 2.0 * eg[me["x"], pl.ds(2 * me["c"], 2)].reshape(32, EXT)
        lora[0] = nn(e2[:, 128:256], cw[...])
        lora[1] = nn(e2[:, 0:128], aw[...])

    pair = [group(4 * 8) for n in range(2)]
    b_x = [group(3 * 8) for n in range(2)]
    accs, res = (acc_o, acc_i), (o_out, o_in)

    def rows_of(xi, c):
        return pl.ds(pl.multiple_of((xi * 2 + c) * 32, 32), 32)

    def pair_send(n):
        for xi in range(X):
            qt[n, xi] = accs[n][rows_of(xi, other), :].astype(BF16)
        put(pair[n], qt.at[n], rt.at[n], {"c": other})

    def x_send(n):
        arrived(pair[n])
        for off in (2, 1, 3):
            xi = at_off("x", off)
            v = accs[n][rows_of(xi, me["c"]), :] + rt[n, xi].astype(F32)
            uq[n, off - 1] = v.astype(BF16)
            put(b_x[n], uq.at[n, off - 1], rx.at[n, off - 1], {"x": xi})

    def x_fin(n):
        v = accs[n][rows_of(me["x"], me["c"]), :] + rt[n, me["x"]].astype(F32) + lora[n]
        arrived(b_x[n])
        for k in range(3):
            v = v + rx[n, k].astype(F32)
        res[n][...] = v.astype(BF16)

    def on_sub(fn):
        return lambda s: fn(bufs[s][8], SUBS[s][0], st[s])

    def on_half(fn):
        return lambda n: fn(halves["zy"[n]], "zy"[n], hst["zy"[n]])

    steps = {"gu": compute_gu, "hb": compute_hb, "sendgu": lambda s: rs1_send(s, slice(0, 2 * SUBS[s][2])),
             "sendhb": lambda s: rs1_send(s, slice(2 * SUBS[s][2], WIDTHS[s])), "agg": rs1_agg, "sum": rs1_fin,
             "mid": middle, "near": near, "spread": on_sub(spread), "fwd": on_sub(forward),
             "fin": lambda s: arrived(st[s]["b"]), "hspread": on_half(spread), "hfwd": on_half(forward),
             "hfin": lambda n: arrived(hst["zy"[n]]["b"]),
             "out": post_o, "in": post_i, "flip": flip, "grad": grads, "hgrad": h_grads,
             "esend": e_send, "esum": e_sum, "emore": e_more, "efin": e_fin,
             "pair": pair_send, "xsend": x_send, "xfin": x_fin}
    for step, s in SCHEDULE:
        with jax.named_scope(step + str(s)):
            steps[step](s)
    pltpu.make_async_copy(bytes_of(SENT_TILES), bytes_of(SENT_TILES), send_sem).wait()
    assert (len(arrivals), moved[0]) == (N_RECV, SENT_TILES), (len(arrivals), moved[0])


RESULTS = (
    ((32, DS), BF16), ((32, DS), BF16), ((2, R, DS), F32),
    ((2, R, FS), F32), ((R, FS), F32), ((R, DS), F32),
)


def store(*refs):
    copies = [pltpu.make_async_copy(refs[n], refs[6 + n], refs[12].at[n]) for n in (3, 4, 2, 5, 0, 1)]
    for c in copies:
        c.start()
    for c in copies:
        c.wait()


def per_device(tok, w, wd, a, b, din, dout, cot):
    at = jnp.swapaxes(a, 1, 2).reshape(2 * R, DS)
    dint = jnp.swapaxes(din, 0, 1)
    vm = pltpu.VMEM
    scratch = [
        vm((2, X * C, 32, DS), BF16), vm((2, DS, FS), BF16), vm((FS, DS), BF16),
        vm((128, DS), BF16), vm((128, DS), BF16), vm((3, 128, FS), BF16),
        vm((T, DS), F32), vm((T, DS), F32),
        vm((16, EXT), BF16), vm((16, EXT), F32), vm((EXT, T), BF16), vm((2, 32, DS), F32),
        vm((2, X, 32, DS), BF16), vm((2, X, 32, DS), BF16),
        vm((2, 3, 32, DS), BF16), vm((2, 3, 32, DS), BF16),
        vm((16, EXT), BF16), vm((7, 16, EXT), BF16), vm((Y, Z, 16, EXT), BF16),
        vm((max(SENT_TILES, LOAD_TILES), 16, 128), BF16),
        vm((Y, Z, 16, HALVES["y"][2]), BF16), vm((Y, Z, 16, HALVES["z"][2]), BF16),
    ]
    for wid, (_, _, hw, _) in zip(WIDTHS, SUBS):
        scratch += [
            vm((Y, Z, 16, wid), F32), vm((Y, Z, 16, wid), BF16),
            vm((2, 2, 16, wid), BF16), vm((2, 2, 16, wid), BF16), vm((2, 4, 16, wid), BF16),
            vm((4, 16, wid), F32), vm((4, 16, wid), BF16), vm((3, 16, wid), BF16),
            vm((Y, Z, 16, 2 * hw), BF16),
        ]
    scratch += [pltpu.SemaphoreType.DMA((3,)), pltpu.SemaphoreType.DMA, pltpu.SemaphoreType.DMA((N_RECV,))]
    anyspec = pl.BlockSpec(memory_space=pltpu.MemorySpace.HBM)
    vspec = pl.BlockSpec(memory_space=pltpu.VMEM)
    res = pl.pallas_call(
        body,
        out_shape=tuple(vm(s, d) for s, d in RESULTS),
        in_specs=[anyspec] * 8,
        out_specs=(vspec,) * 6,
        scratch_shapes=scratch,
        compiler_params=pltpu.CompilerParams(
            collective_id=0, has_side_effects=True, vmem_limit_bytes=40 * 1024 * 1024),
        name="layer",
    )(*(pltpu.with_memory_space_constraint(v, pltpu.MemorySpace.HBM)
        for v in (tok, w, wd, at, b, dint, dout, cot)))
    out, inp, gl, gf, di, do = pl.pallas_call(
        store,
        out_shape=tuple(jax.ShapeDtypeStruct(s, d) for s, d in RESULTS),
        in_specs=[vspec] * 6,
        out_specs=(anyspec,) * 6,
        scratch_shapes=[pltpu.SemaphoreType.DMA((6,))],
        compiler_params=pltpu.CompilerParams(vmem_limit_bytes=1024 * 1024),
        name="store",
    )(*res)
    return out, inp, jnp.swapaxes(gl, 1, 2), gf, jnp.swapaxes(di, 0, 1), do


def solution(mesh):
    torus = Mesh(mesh.devices.reshape(X, C, Y, Z), ("x", "c", "y", "z"))
    dp, mp = ("x", "c"), ("y", "z")
    in_specs = (
        P(dp, mp), P(None, mp, dp), P(dp, mp), P(None, mp, None),
        P(None, None, dp), P(dp, None), P(None, mp), P(dp, mp),
    )
    out_specs = (P(dp, mp), P(dp, mp), P(None, mp, None), P(None, None, dp), P(dp, None), P(None, mp))
    return jax.shard_map(per_device, mesh=torus, in_specs=in_specs, out_specs=out_specs, check_vma=False)
```

time: 61.7 us -> 59.4 us (0.963)
  Pallas kernels: 60.9 us -> 58.7 us
    pallas_call x1, Pallas kernels: 59.6 us -> 57.4 us  [per_device(): pl.pallas_call(body, out_shape=tuple((vm(s, d) for s, d in RESULTS)), in_...]
where the time goes in v3:
time: 59.4 us; the launch traced here: 59.3 us
  Pallas kernels  58.7 us (99%)
  between operations  0.64 us (1%)
    pallas_call x1, Pallas kernels, per_device(): pl.pallas_call(body, out_shape=tuple((vm(s, d) for s, d in RESULTS)), in_...  57.4 us
    pallas_call x1, Pallas kernels, per_device(): pl.pallas_call(store, out_shape=tuple((jax.ShapeDtypeStruct(s, d) for s,...  1.3 us

profile of v3, /device:TPU:1, one launch (start us, length us, event | category | flops | bytes accessed | tf_op | source)
XLA Modules:
  0.0 59.3 jit_solution(8271236384600071824)
XLA Ops:
  0.6 57.4 %layer.1 = (bf16[32,512]{1,0:T(8,128)(2,1)S(1)}, bf16[32,512]{1,0:T(8,128)(2,1)S(1)}, f32[2,64,512]{2,1,0:T(8,128)S(1)}, f32[2,64,1920]{2,1,0:T(8,128)S(1)}, f32...) custom-call(bf16[32,512]{1,0:T(8,128)(2,1)} %tok.1, bf16[2,512,1920]{2,1,0:T(8,128)(2,1)} %w_hbm.1, bf16[1920,512]{1,0:T(8,128)(2,1)} %wd_hbm.1, ...), custom_call_target="tpu_custom_call" | custom-call | tf_op jit(solution)/shard_map/layer/pallas_call | solution.py:442
  58.0 1.3 %store.1 = (bf16[32,512]{1,0:T(8,128)(2,1)}, bf16[32,512]{1,0:T(8,128)(2,1)}, f32[2,64,512]{2,1,0:T(8,128)}, f32[2,64,1920]{2,1,0:T(8,128)}, f32[64,1920]{1,0:T(8,128)}, /*index=5*/f32[64,512]{1,0:T(8,128)}) custom-call(bf16[32,512]{1,0:T(8,128)(2,1)S(1)} %get-tuple-element.18.refs_0_, bf16[32,512]{1,0:T(8,128)(2,1)S(1)} %get-tuple-element.19.refs_1_, ...), custom_call_target="tpu_custom_call" | custom-call | tf_op jit(solution)/shard_map/store/pallas_call | solution.py:453

commit v4 on v3

--- a/solution.py
+++ b/solution.py
@@ -27,7 +27,7 @@
 WIDTHS = tuple(3 * hw + (EXT if ext else 0) for _, _, hw, ext in SUBS)
 HALVES = {"y": (0, 1024, 1024), "z": (1024, 896, 896 + EXT)}
 NS = len(SUBS)
-N_RECV = 17 + 6 * NS
+N_RECV = 17 + 4 * NS
 TILE = 16 * 128
 SENT_TILES = 30 * sum(WIDTHS) // 128 + 268
 LOAD_TILES = (3 * R * DS + 3 * R * FS + 3 * DS * FS) // TILE
@@ -40,12 +40,12 @@
 SCHEDULE = (
     steps_of(range(3), "gu", "sendgu") + steps_of(range(3), "hb", "sendhb")
     + steps_of(range(3, NS), "gu", "sendgu", "hb", "sendhb")
-    + steps_of(range(NS), "agg") + steps_of(range(NS), "sum") + steps_of(range(NS), "mid", "near")
+    + steps_of(range(NS), "agg") + steps_of(range(NS), "sum") + steps_of(range(NS), "mid")
     + [("esend", 0)] + steps_of(range(4), "spread") + steps_of(range(2), "hspread") + steps_of(range(4, 6), "spread")
     + steps_of(range(2), "hfwd") + steps_of(range(6, NS), "spread") + steps_of(range(4), "fwd")
     + [("esum", 0)] + steps_of(range(4, 6), "fwd")
-    + [("hfin", 0), ("hfin", 1), ("out", 0), ("pair", 0)]
-    + steps_of(range(6, NS), "fwd") + steps_of(range(2), "fin", "in") + [("xsend", 0)]
+    + [("hfin", 0), ("hfin", 1)] + steps_of(range(6, NS), "fwd") + [("out", 0), ("pair", 0)]
+    + steps_of(range(2), "fin", "in") + [("xsend", 0)]
     + steps_of(range(2, 4), "fin", "in") + [("emore", 0)]
     + steps_of(range(4, NS), "fin", "in") + [("pair", 1), ("flip", 0), ("hgrad", 0)]
     + steps_of(range(3), "grad") + [("xsend", 1)] + steps_of(range(3, NS), "grad")
@@ -79,19 +79,21 @@
     def bytes_of(tiles):
         return bytes_ref.at[0:tiles]
 
-    def group(like):
+    def group(like, same=None):
+        if same is not None:
+            return same[0], like
         arrivals.append(like)
-        return len(arrivals) - 1
+        return len(arrivals) - 1, like
 
     def put(g, src, dst, device):
         moved[0] += math.prod(src.shape) // TILE
         pltpu.make_async_remote_copy(
-            src_ref=src, dst_ref=dst, send_sem=send_sem, recv_sem=recv_sem.at[g],
+            src_ref=src, dst_ref=dst, send_sem=send_sem, recv_sem=recv_sem.at[g[0]],
             device_id=device, device_id_type=MESH).start()
 
     def arrived(g):
-        size = bytes_of(arrivals[g])
-        pltpu.make_async_copy(size, size, recv_sem.at[g]).wait()
+        size = bytes_of(g[1])
+        pltpu.make_async_copy(size, size, recv_sem.at[g[0]]).wait()
 
     other = 1 - me["c"]
     barrier = pltpu.get_barrier_semaphore()
@@ -181,8 +183,9 @@
     st = []
     for s in range(NS):
         n, g = WIDTHS[s] // 128, 2 * SUBS[s][2] // 128
-        st.append({"t": group(4 * n), "f": group(8 * n), "r": group(3 * n),
-                   "a": group(3 * g), "t2": group(4 * g), "b": group(8 * g)})
+        t, f = group(4 * n), group(8 * n)
+        st.append({"t": t, "f": f, "r": group(3 * n), "a": group(3 * g, f),
+                   "t2": group(4 * g, t), "b": group(8 * g)})
 
     halves = {"y": h_y, "z": h_z}
     hst = {}
@@ -264,12 +267,12 @@
             mine = hid_ref.at[my[0], my[1], :, piece]
             for off in (2, 1, 3):
                 put(hst[a]["a"], mine, mine, {b: at_off(b, off)})
+        near(s)
         add(e_acc.at[:, 0:128], "bl", nt(gb, ew[0, :, cols]) + nt(ub, ew[1, :, cols]))
         add(e_acc.at[:, 128:256], "ld", nt(hid, ew[2, :, cols]))
 
     def near(s):
-        b = other_axis[SUBS[s][0]]
-        mine = bufs[s][8].at[me["y"], me["z"]]
+        b, mine = other_axis[SUBS[s][0]], bufs[s][8].at[me["y"], me["z"]]
         for off in (2, 1, 3):
             put(st[s]["a"], mine, mine, {b: at_off(b, off)})
 
@@ -387,7 +390,7 @@
 
     steps = {"gu": compute_gu, "hb": compute_hb, "sendgu": lambda s: rs1_send(s, slice(0, 2 * SUBS[s][2])),
              "sendhb": lambda s: rs1_send(s, slice(2 * SUBS[s][2], WIDTHS[s])), "agg": rs1_agg, "sum": rs1_fin,
-             "mid": middle, "near": near, "spread": on_sub(spread), "fwd": on_sub(forward),
+             "mid": middle, "spread": on_sub(spread), "fwd": on_sub(forward),
              "fin": lambda s: arrived(st[s]["b"]), "hspread": on_half(spread), "hfwd": on_half(forward),
              "hfin": lambda n: arrived(hst["zy"[n]]["b"]),
              "out": post_o, "in": post_i, "flip": flip, "grad": grads, "hgrad": h_grads,

time: 59.4 us -> 59 us (level)
  no operation moved by 1% of the time
where the time goes in v4:
time: 59 us; the launch traced here: 58.9 us
  Pallas kernels  58.3 us (99%)
  between operations  0.64 us (1%)
    pallas_call x1, Pallas kernels, per_device(): pl.pallas_call(body, out_shape=tuple((vm(s, d) for s, d in RESULTS)), in_...  57 us
    pallas_call x1, Pallas kernels, per_device(): pl.pallas_call(store, out_shape=tuple((jax.ShapeDtypeStruct(s, d) for s,...  1.3 us

profile of v4, /device:TPU:1, one launch (start us, length us, event | category | flops | bytes accessed | tf_op | source)
XLA Modules:
  0.0 58.9 jit_solution(15337407155006095662)
XLA Ops:
  0.6 57.0 %layer.1 = (bf16[32,512]{1,0:T(8,128)(2,1)S(1)}, bf16[32,512]{1,0:T(8,128)(2,1)S(1)}, f32[2,64,512]{2,1,0:T(8,128)S(1)}, f32[2,64,1920]{2,1,0:T(8,128)S(1)}, f32...) custom-call(bf16[32,512]{1,0:T(8,128)(2,1)} %tok.1, bf16[2,512,1920]{2,1,0:T(8,128)(2,1)} %w_hbm.1, bf16[1920,512]{1,0:T(8,128)(2,1)} %wd_hbm.1, ...), custom_call_target="tpu_custom_call" | custom-call | tf_op jit(solution)/shard_map/layer/pallas_call | solution.py:445
  57.6 1.3 %store.1 = (bf16[32,512]{1,0:T(8,128)(2,1)}, bf16[32,512]{1,0:T(8,128)(2,1)}, f32[2,64,512]{2,1,0:T(8,128)}, f32[2,64,1920]{2,1,0:T(8,128)}, f32[64,1920]{1,0:T(8,128)}, /*index=5*/f32[64,512]{1,0:T(8,128)}) custom-call(bf16[32,512]{1,0:T(8,128)(2,1)S(1)} %get-tuple-element.18.refs_0_, bf16[32,512]{1,0:T(8,128)(2,1)S(1)} %get-tuple-element.19.refs_1_, ...), custom_call_target="tpu_custom_call" | custom-call | tf_op jit(solution)/shard_map/store/pallas_call | solution.py:456

commit v5 on v4

--- a/solution.py
+++ b/solution.py
@@ -38,7 +38,8 @@
 
 
 SCHEDULE = (
-    steps_of(range(3), "gu", "sendgu") + steps_of(range(3), "hb", "sendhb")
+    [("gate", 1), ("sendgate", 1), ("gu", 0), ("sendgu", 0), ("up", 1), ("sendup", 1), ("gu", 2), ("sendgu", 2)]
+    + steps_of((1, 0, 2), "hb", "sendhb")
     + steps_of(range(3, NS), "gu", "sendgu", "hb", "sendhb")
     + steps_of(range(NS), "agg") + steps_of(range(NS), "sum") + steps_of(range(NS), "mid")
     + [("esend", 0)] + steps_of(range(4), "spread") + steps_of(range(2), "hspread") + steps_of(range(4, 6), "spread")
@@ -151,10 +152,10 @@
         bufs[s][0][:, :, :, cols] = v
         bufs[s][1][:, :, :, cols] = v.astype(BF16)
 
-    def compute_gu(s):
+    def compute_gu(s, which=(0, 1)):
         _, f0, hw, _ = SUBS[s]
         cols = slice(f0, f0 + hw)
-        for n in range(2):
+        for n in which:
             keep(s, seg(n, hw), nn(rows_all(0), w[n, :, cols]))
 
     def compute_hb(s):
@@ -388,7 +389,9 @@
     def on_half(fn):
         return lambda n: fn(halves["zy"[n]], "zy"[n], hst["zy"[n]])
 
-    steps = {"gu": compute_gu, "hb": compute_hb, "sendgu": lambda s: rs1_send(s, slice(0, 2 * SUBS[s][2])),
+    steps = {"gate": lambda s: compute_gu(s, (0,)), "up": lambda s: compute_gu(s, (1,)),
+             "sendgate": lambda s: rs1_send(s, seg(0, SUBS[s][2])), "sendup": lambda s: rs1_send(s, seg(1, SUBS[s][2])),
+             "gu": compute_gu, "hb": compute_hb, "sendgu": lambda s: rs1_send(s, slice(0, 2 * SUBS[s][2])),
              "sendhb": lambda s: rs1_send(s, slice(2 * SUBS[s][2], WIDTHS[s])), "agg": rs1_agg, "sum": rs1_fin,
              "mid": middle, "spread": on_sub(spread), "fwd": on_sub(forward),
              "fin": lambda s: arrived(st[s]["b"]), "hspread": on_half(spread), "hfwd": on_half(forward),

time: 59 us -> 59.1 us (level)
  no operation moved by 1% of the time
where the time goes in v5:
time: 59.1 us; the launch traced here: 59 us
  Pallas kernels  58.4 us (99%)
  between operations  0.64 us (1%)
    pallas_call x1, Pallas kernels, per_device(): pl.pallas_call(body, out_shape=tuple((vm(s, d) for s, d in RESULTS)), in_...  57.1 us
    pallas_call x1, Pallas kernels, per_device(): pl.pallas_call(store, out_shape=tuple((jax.ShapeDtypeStruct(s, d) for s,...  1.3 us

profile of v5, /device:TPU:1, one launch (start us, length us, event | category | flops | bytes accessed | tf_op | source)
XLA Modules:
  0.0 59.0 jit_solution(16507398755236255937)
XLA Ops:
  0.6 57.1 %layer.1 = (bf16[32,512]{1,0:T(8,128)(2,1)S(1)}, bf16[32,512]{1,0:T(8,128)(2,1)S(1)}, f32[2,64,512]{2,1,0:T(8,128)S(1)}, f32[2,64,1920]{2,1,0:T(8,128)S(1)}, f32...) custom-call(bf16[32,512]{1,0:T(8,128)(2,1)} %tok.1, bf16[2,512,1920]{2,1,0:T(8,128)(2,1)} %w_hbm.1, bf16[1920,512]{1,0:T(8,128)(2,1)} %wd_hbm.1, ...), custom_call_target="tpu_custom_call" | custom-call | tf_op jit(solution)/shard_map/layer/pallas_call | solution.py:448
  57.7 1.3 %store.1 = (bf16[32,512]{1,0:T(8,128)(2,1)}, bf16[32,512]{1,0:T(8,128)(2,1)}, f32[2,64,512]{2,1,0:T(8,128)}, f32[2,64,1920]{2,1,0:T(8,128)}, f32[64,1920]{1,0:T(8,128)}, /*index=5*/f32[64,512]{1,0:T(8,128)}) custom-call(bf16[32,512]{1,0:T(8,128)(2,1)S(1)} %get-tuple-element.18.refs_0_, bf16[32,512]{1,0:T(8,128)(2,1)S(1)} %get-tuple-element.19.refs_1_, ...), custom_call_target="tpu_custom_call" | custom-call | tf_op jit(solution)/shard_map/store/pallas_call | solution.py:459
